TPU v7x, 128 devices: a whole 4x4x4 slice. The times are simulated.
128 devices in a mesh: dp: 1, sp: 64 (over z, y, x), tp: 2 (over core).
Axes of the slice: x: 4, y: 4, z: 4, core: 2. Of those that a mesh axis runs over, the one named last changes fastest.
Arguments:
- x_in: bfloat16 [16, 3072, 56, 64], P('dp', 'sp', None, 'tp')
- act_saved: bfloat16 [16, 3072, 56, 64], P('dp', 'sp', None, 'tp')
- w_one: bfloat16 [3, 3, 64, 64], P(None, None, 'tp')
- w_two: bfloat16 [3, 3, 64, 64], P(None, None, 'tp')
- d_out: bfloat16 [16, 3072, 56, 64], P('dp', 'sp', None, 'tp')
Outputs:
- output 1: bfloat16 [16, 3072, 56, 64], P('dp', 'sp', None, 'tp')
- output 2: float32 [3, 3, 64, 64], P('dp', None, 'tp')
- output 3: float32 [3, 3, 64, 64], P('dp', None, 'tp')
- output 4: float32 [64], P(('dp', 'tp'))
All inputs are finite; a program needn't handle non-finite values.
Results may differ from a plain program's by a relative error of at most 0.001.
Values are sent between devices in bfloat16 or wider.
A program may use at most 1 GiB of HBM per device.

v0:
```python
import jax
import jax.numpy as jnp
from jax import lax
from jax.sharding import PartitionSpec as P


def conv_rows(padded, kernel):
    return lax.conv_general_dilated(padded, kernel[::-1, ::-1], (1, 1), ((0, 0), (1, 1)), dimension_numbers=("NHWC", "HWOI", "NHWC"), preferred_element_type=jnp.float32)


def weight_grad(padded, image):
    corr = lax.conv_general_dilated(padded, image, (1, 1), ((0, 0), (1, 1)), dimension_numbers=("CHWN", "IHWO", "HWCN"), preferred_element_type=jnp.float32)
    return corr[::-1, ::-1]


def solution(mesh):
    row_devs = mesh.shape["sp"]
    to_next = [(dev_index, dev_index + 1) for dev_index in range(row_devs - 1)]
    to_prev = [(dev_index + 1, dev_index) for dev_index in range(row_devs - 1)]

    def with_halo(tile):
        above = lax.ppermute(tile[:, -1:], "sp", to_next)
        below = lax.ppermute(tile[:, :1], "sp", to_prev)
        return jnp.concatenate([above, tile, below], axis=1)

    def local_step(x_in, act_saved, w_one, w_two, d_out):
        dy_pad = lax.all_gather(with_halo(d_out), "tp", axis=3, tiled=True)
        d_act = conv_rows(dy_pad, w_two)
        grad_two = lax.psum(weight_grad(dy_pad, act_saved), "sp")
        masked = jnp.where(act_saved > 0, d_act, 0.0)
        grad_bias = lax.psum(jnp.sum(masked, axis=(0, 1, 2)), "sp")
        dz_pad = lax.all_gather(with_halo(masked.astype(jnp.bfloat16)), "tp", axis=3, tiled=True)
        d_x = (d_out.astype(jnp.float32) + conv_rows(dz_pad, w_one)).astype(jnp.bfloat16)
        grad_one = lax.psum(weight_grad(dz_pad, x_in), "sp")
        return d_x, grad_one, grad_two, grad_bias

    act_spec = P("dp", "sp", None, "tp")
    kern_spec = P(None, None, "tp", None)
    grad_spec = P("dp", None, "tp", None)
    return jax.shard_map(local_step, mesh=mesh, in_specs=(act_spec, act_spec, kern_spec, kern_spec, act_spec), out_specs=(act_spec, grad_spec, grad_spec, P(("dp", "tp"))), check_vma=False)
```

profile of v0, /device:TPU:0, one launch (start us, length us, event | category | flops | bytes accessed | tf_op | source)
XLA Modules:
  0.0 563.2 jit_solution(6714142899814117324)
XLA Ops:
  7.2 6.8 %copy.19 = bf16[16,48,56,32]{2,0,1,3:T(8,128)(2,1)S(1)} copy(bf16[16,48,56,32]{2,3,1,0:T(8,128)(2,1)} %param.9) | data formatting | bytes 5505024 | tf_op args[4]
  14.1 3.5 collective-permute-start
  17.6 1.3 collective-permute-start.1
  18.9 1.4 collective-permute-done
  20.4 4.2 collective-permute-done.1
  24.5 4.7 pad_maximum_fusion.1
  29.2 0.2 all-gather.5.cloned.1.call-start
  29.4 13.6 %copy.18 = bf16[16,48,56,32]{3,0,2,1:T(8,128)(2,1)} copy(bf16[16,48,56,32]{2,3,1,0:T(8,128)(2,1)} %param.6) | data formatting | bytes 5505024 | tf_op args[1]
  43.0 20.9 %all-gather.3.cloned.1.call-done = bf16[16,50,56,64]{2,0,1,3:T(8,128)(2,1)} async-done(((bf16[16,50,56,32]{2,0,1,3:T(8,128)(2,1)}), bf16[16,50,56,64]{2,0,1,3:T(8,128)(2,1)}) %all-gather.3.cloned.1.call-update) | async-done | bytes 5734416 | tf_op jit(solution)/shard_map/all_gather | solution.py:27
  63.9 22.1 %copy.22 = bf16[16,50,56,64]{3,0,2,1:T(8,128)(2,1)} copy(bf16[16,50,56,64]{2,0,1,3:T(8,128)(2,1)} %all-gather.3.cloned.1.call-done) | data formatting | bytes 11468800 | tf_op jit(solution)/shard_map/all_gather | solution.py:27
  86.0 30.7 %fusion.1 = (bf16[16,48,56,32]{3,0,2,1:T(8,128)(2,1)S(1)}, f32[16,48,56,32]{3,0,2,1:T(8,128)}) fusion(bf16[16,48,56,32]{3,0,2,1:T(8,128)(2,1)} %copy.18, bf16[16,50,56,64]{3,0,2,1:T(8,128)(2,1)} %copy.22, bf16[3,3,32,64]{3,2,1,0:T(8,128)(2,1)S(1)} %copy-done), kind=kOutput, calls=%fused_computation.3 | convolution fusion | flops 1572077568 | bytes 16781312 | tf_op jit(solution)/shard_map/conv_general_dilated | solution.py:8
  116.7 3.5 collective-permute-start.2
  120.2 1.3 collective-permute-start.3
  121.5 4.0 collective-permute-done.2
  125.5 4.1 collective-permute-done.3
  129.6 6.2 %pad_maximum_fusion = bf16[16,50,56,32]{3,0,2,1:T(8,128)(2,1)} fusion(bf16[16,1,56,32]{3,0,2,1:T(8,128)(2,1)S(1)} %collective-permute-done.3, bf16[16,48,56,32]{3,0,2,1:T(8,128)(2,1)S(1)} %get-tuple-element.18, bf16[16,1,56,32]{3,0,2,1:T(8,128)(2,1)S(1)} %collective-permute-done.2), kind=kLoop, calls=%fused_computation.4 | loop fusion | flops 2867200 | bytes 5734400 | tf_op jit(solution)/shard_map/concatenate | solution.py:24
  135.8 18.6 %copy.23 = bf16[16,50,56,32]{2,0,1,3:T(8,128)(2,1)} copy(bf16[16,50,56,32]{3,0,2,1:T(8,128)(2,1)} %pad_maximum_fusion) | data formatting | bytes 5734400 | tf_op jit(solution)/shard_map/concatenate | solution.py:24
  154.4 0.3 all-reduce.3.cloned.1.call-start
  154.7 13.6 %copy.17 = bf16[16,48,56,32]{3,0,2,1:T(8,128)(2,1)} copy(bf16[16,48,56,32]{2,3,1,0:T(8,128)(2,1)} %param.9) | data formatting | bytes 5505024 | tf_op args[4]
  168.3 13.7 %copy.26 = bf16[16,48,56,32]{3,0,2,1:T(8,128)(2,1)} copy(bf16[16,48,56,32]{2,3,1,0:T(8,128)(2,1)} %param.5) | data formatting | bytes 5505024 | tf_op args[0]
  182.0 17.4 %fusion.5 = f32[3,3,32,64]{3,2,1,0:T(8,128)S(1)} fusion(bf16[16,50,56,64]{3,0,2,1:T(8,128)(2,1)} %copy.22, bf16[16,48,56,32]{3,0,2,1:T(8,128)(2,1)} %copy.18), kind=kOutput, calls=%fused_computation.9 | convolution fusion | flops 1566572544 | bytes 8560640 | tf_op jit(solution)/shard_map/conv_general_dilated | solution.py:12
  199.4 0.7 rev.9
  200.1 12.6 %fusion = f32[32]{0:T(128)S(1)} fusion(f32[16,48,56,32]{3,0,2,1:T(8,128)} %get-tuple-element.19, bf16[16,48,56,32]{3,0,2,1:T(8,128)(2,1)} %copy.18), kind=kLoop, calls=%fused_computation.2 | loop fusion | flops 4128736 | bytes 8257664 | tf_op jit(solution)/shard_map/reduce_sum | solution.py:31
  212.7 177.8 %psum.23 = f32[32]{0:T(128)} all-reduce(f32[32]{0:T(128)S(1)} %fusion), channel_id=1, replica_groups=mesh['dp'=1,'sp'=64,'tp'=2] {'sp'}, use_global_device_ids=true, to_apply=%region_3.4 | all-reduce | flops 32 | bytes 256 | tf_op jit(solution)/shard_map/psum | solution.py:31
  390.5 22.1 %copy.24 = bf16[16,50,56,64]{3,0,2,1:T(8,128)(2,1)} copy(bf16[16,50,56,64]{2,0,1,3:T(8,128)(2,1)} %all-gather.5.cloned.1.call-done) | data formatting | bytes 11468800 | tf_op jit(solution)/shard_map/all_gather | solution.py:32
  412.6 17.5 %fusion.4 = f32[3,3,32,64]{3,2,1,0:T(8,128)S(1)} fusion(bf16[16,50,56,64]{3,0,2,1:T(8,128)(2,1)} %copy.24, bf16[16,48,56,32]{3,0,2,1:T(8,128)(2,1)} %copy.26), kind=kOutput, calls=%fused_computation.8 | convolution fusion | flops 1566572544 | bytes 8560640 | tf_op jit(solution)/shard_map/conv_general_dilated | solution.py:12
  430.0 0.7 rev.8
  430.7 30.1 %add_convert_fusion = bf16[16,48,56,32]{3,0,2,1:T(8,128)(2,1)} fusion(bf16[16,48,56,32]{3,0,2,1:T(8,128)(2,1)} %copy.17, bf16[16,50,56,64]{3,0,2,1:T(8,128)(2,1)} %copy.24, bf16[3,3,32,64]{3,2,1,0:T(8,128)(2,1)S(1)} %copy-done.2), kind=kOutput, calls=%fused_computation | convolution fusion | flops 1570701312 | bytes 11276288 | tf_op jit(solution)/shard_map/conv_general_dilated | solution.py:8
  460.9 13.2 %copy.29 = bf16[16,48,56,32]{2,3,1,0:T(8,128)(2,1)} copy(bf16[16,48,56,32]{3,0,2,1:T(8,128)(2,1)} %add_convert_fusion) | data formatting | bytes 5505024
  474.1 79.4 %all-reduce.3.cloned.1.call-done = (f32[3,3,32,64]{3,2,1,0:T(8,128)}, f32[3,3,32,64]{3,2,1,0:T(8,128)}) async-done(((f32[3,3,32,64]{3,2,1,0:T(8,128)}, f32[3,3,32,64]{3,2,1,0:T(8,128)}), (f32[3,3,32,64]{3,2,1,0:T(8,128)}, f32[3,3,32,64]{3,2,1,0:T(8,128)})) %all-reduce.3.cloned.1.call-update) | async-done | bytes 147472 | tf_op jit(solution)/shard_map/psum | solution.py:34
  553.6 1.6 copy.32
  555.1 1.6 copy.33
  (13 shorter events, 0.2 us)
Async XLA Ops:
  7.2 78.8 %copy-start = (bf16[3,3,32,64]{3,2,1,0:T(8,128)(2,1)S(1)}, bf16[3,3,32,64]{3,2,1,0:T(8,128)(2,1)}, u32[]{:S(2)}) copy-start(bf16[3,3,32,64]{3,2,1,0:T(8,128)(2,1)} %param.8) | copy-start | bytes 110596
  7.2 56.7 %all-gather.3.cloned.1.call-start = ((), (), s32[]{:S(2)}) async-start(), calls=%async_computation | async-start | bytes 19660800 | tf_op jit(solution)/shard_map/all_gather | solution.py:27
  14.1 6.3 %collective-permute-start = (bf16[16,1,56,32]{2,0,1,3:T(8,128)(2,1)S(1)}, bf16[16,1,56,32]{2,0,1,3:T(8,128)(2,1)S(1)}, u32[]{:S(2)}, u32[]{:S(2)}) collective-permute-start(bf16[16,1,56,32]{2,0,1,3:T(8,128)(2,1)S(1)} %get-tuple-element.16), channel_id=1, source_target_pairs={{0,2},{2,4},{4,6},{6,8},{8,10},{10,12},{12,14},{14,16},{16,18},{18... | collective-permute-start | bytes 172040 | tf_op jit(solution)/shard_map/ppermute | solution.py:22
  17.6 6.9 %collective-permute-start.1 = (bf16[16,1,56,32]{2,0,1,3:T(8,128)(2,1)S(1)}, bf16[16,1,56,32]{2,0,1,3:T(8,128)(2,1)S(1)}, u32[]{:S(2)}, u32[]{:S(2)}) collective-permute-start(bf16[16,1,56,32]{2,0,1,3:T(8,128)(2,1)S(1)} %get-tuple-element.17), channel_id=1, source_target_pairs={{2,0},{4,2},{6,4},{8,6},{10,8},{12,10},{14,12},{16,14},{18,16},{20... | collective-permute-start | bytes 172040 | tf_op jit(solution)/shard_map/ppermute | solution.py:23
  29.2 361.3 %all-gather.5.cloned.1.call-start = ((), (), s32[]{:S(2)}) async-start(), calls=%async_computation.1 | async-start | bytes 19660800 | tf_op jit(solution)/shard_map/all_gather | solution.py:32
  116.7 8.8 %collective-permute-start.2 = (bf16[16,1,56,32]{3,0,2,1:T(8,128)(2,1)S(1)}, bf16[16,1,56,32]{3,0,2,1:T(8,128)(2,1)S(1)}, u32[]{:S(2)}, u32[]{:S(2)}) collective-permute-start(bf16[16,1,56,32]{3,0,2,1:T(8,128)(2,1)S(1)} %get-tuple-element.14), channel_id=1, source_target_pairs={{0,2},{2,4},{4,6},{6,8},{8,10},{10,12},{12,14},{14,16},{16,18},{18... | collective-permute-start | bytes 172040 | tf_op jit(solution)/shard_map/ppermute | solution.py:22
  120.2 9.4 %collective-permute-start.3 = (bf16[16,1,56,32]{3,0,2,1:T(8,128)(2,1)S(1)}, bf16[16,1,56,32]{3,0,2,1:T(8,128)(2,1)S(1)}, u32[]{:S(2)}, u32[]{:S(2)}) collective-permute-start(bf16[16,1,56,32]{3,0,2,1:T(8,128)(2,1)S(1)} %get-tuple-element.15), channel_id=1, source_target_pairs={{2,0},{4,2},{6,4},{8,6},{10,8},{12,10},{14,12},{16,14},{18,16},{20... | collective-permute-start | bytes 172040 | tf_op jit(solution)/shard_map/ppermute | solution.py:23
  154.4 399.1 %all-reduce.3.cloned.1.call-start = ((), (), s32[]{:S(2)}) async-start(), calls=%async_computation.2 | async-start | bytes 589824 | tf_op jit(solution)/shard_map/psum | solution.py:34
  412.6 18.2 %copy-start.2 = (bf16[3,3,32,64]{3,2,1,0:T(8,128)(2,1)S(1)}, bf16[3,3,32,64]{3,2,1,0:T(8,128)(2,1)}, u32[]{:S(2)}) copy-start(bf16[3,3,32,64]{3,2,1,0:T(8,128)(2,1)} %param.7) | copy-start | bytes 110596
  430.7 126.0 %copy-start.1 = (bf16[3,3,32,64]{3,2,1,0:T(8,128)(2,1)S(1)}, bf16[3,3,32,64]{3,2,1,0:T(8,128)(2,1)}, u32[]{:S(2)}) copy-start(bf16[3,3,32,64]{3,2,1,0:T(8,128)(2,1)} %param.8) | copy-start | bytes 110596
Sparse Core Ops, SparseCore 0:
  29.3 34.5 all-gather.2
  154.5 34.0 all-gather.4
  430.8 122.6 all-reduce.2
where the time goes:
time: 566 us; the launch traced here: 563 us
  blocking collectives  178 us (31%)
  local copies, waits for them, and re-layouts  128 us (23%)
  waiting for transfers between devices  114 us (20%)
  matrix products  95.7 us (17%)
  other arithmetic  23.5 us (4%)
  between operations  13.8 us (2%)
  starting transfers between devices  10.1 us (2%)
    psum x1, blocking collectives, local_step(): grad_bias = lax.psum(jnp.sum(masked, axis=(0, 1, 2)), 'sp')  178 us
    psum x1, waiting for transfers between devices, local_step(): grad_one = lax.psum(weight_grad(dz_pad, x_in), 'sp')  79.4 us
    unnamed x13, local copies, waits for them, and re-layouts  64.1 us
    conv_general_dilated x2, matrix products, conv_rows(): lax.conv_general_dilated(padded, kernel[::-1, ::-1], (1, 1), ((0, 0), (1,...  60.8 us
    conv_general_dilated x2, matrix products, weight_grad(): lax.conv_general_dilated(padded, image, (1, 1), ((0, 0), (1, 1)), dimensi...  34.9 us
    all_gather x1, local copies, waits for them, and re-layouts, local_step(): dy_pad = lax.all_gather(with_halo(d_out), 'tp', axis=3, tiled=True)  22.1 us
    all_gather x1, local copies, waits for them, and re-layouts, local_step(): lax.all_gather(with_halo(masked.astype(jnp.bfloat16)), 'tp', axis=3, tile...  22.1 us
    all_gather x1, waiting for transfers between devices, local_step(): dy_pad = lax.all_gather(with_halo(d_out), 'tp', axis=3, tiled=True)  20.9 us
  transfers between devices with their start and end apart: 7, of which 6 were waited for; matrix products, arithmetic and copies ran while one was open for 20% of the time, Pallas kernels for 0%

commit v1 on v0

v1 whole, which is shorter than its diff:
```python
import functools

import jax
import jax.numpy as jnp
from jax import lax
from jax.experimental import pallas as pl
from jax.experimental.pallas import tpu as pltpu
from jax.sharding import PartitionSpec as P

MESH = pl.DeviceIdType.MESH
BF16 = jnp.bfloat16
F32 = jnp.float32


def body(side, rows, chunk, x_hbm, a_hbm, g_hbm, w_one, w_two, dx_hbm, dw_one, dw_two, dbias,
         raw_g, raw_a, raw_x, g_all, z_all, a_pk, x_pk, wm_one, wm_two, acc, bacc, red,
         load_sem, out_sem, gx_send, gx_recv, gh_send, gh_recv, zx_send, zx_recv, zh_send, zh_recv,
         ar_send, ar_recv):
    sp = lax.axis_index("sp")
    tp = lax.axis_index("tp")
    row_devs = side * side * side
    n_chunks = rows // chunk
    n_blocks = rows // 2
    coords = (lax.rem(sp, side), lax.rem(lax.div(sp, side), side), lax.div(sp, side * side))
    strides = (1, side, side * side)
    nxt = lax.rem(sp + 1, row_devs)
    prv = lax.rem(sp + row_devs - 1, row_devs)
    other = 1 - tp
    mine = pl.ds(pl.multiple_of(tp * 32, 32), 32)
    theirs = pl.ds(pl.multiple_of(other * 32, 32), 32)

    def ring_peer(axis, k):
        me = coords[axis]
        return sp + (lax.rem(me + k, side) - me) * strides[axis]

    order = [0] + ([n_chunks - 1] if n_chunks > 1 else []) + list(range(1, n_chunks - 1))

    def load(i, c):
        src = (g_hbm, a_hbm, x_hbm)[i]
        dst = (raw_g, raw_a, raw_x)[i]
        return pltpu.make_async_copy(src.at[:, pl.ds(c * chunk, chunk)], dst.at[:, pl.ds(c * chunk, chunk)], load_sem.at[i, c])

    for i in range(3):
        for c in order:
            load(i, c).start()

    barrier = pltpu.get_barrier_semaphore()
    targets = [(sp, other), (nxt, tp), (nxt, other), (prv, tp), (prv, other)]
    for axis in range(3):
        for k in range(1, side):
            targets.append((ring_peer(axis, k), tp))
    for s, t in targets:
        pl.semaphore_signal(barrier, inc=1, device_id={"sp": s, "tp": t}, device_id_type=MESH)

    for w_ref, wm in ((w_two, wm_two), (w_one, wm_one)):
        wm[...] = jnp.zeros_like(wm)
        for kw in range(3):
            for r in range(2):
                blocks = []
                for rr in range(4):
                    kh = r + 2 - rr
                    blocks.append(w_ref[kh, kw] if 0 <= kh < 3 else jnp.zeros((32, 64), BF16))
                wm[pl.ds(kw * 64 + r * 32, 32), :] = jnp.concatenate(blocks, axis=1)

    def pack(raw, dst, lo, off, sl):
        def step(h, carry):
            for j in range(8):
                left = raw[j, h]
                right = raw[j + 8, h]
                gap = jnp.zeros((32, 8), BF16)
                dst[h + off, sl, pl.ds(j * 128, 128)] = jnp.concatenate([left, gap, right, gap], axis=1)
            return carry
        lax.fori_loop(lo, lo + chunk, step, 0)

    def remote(ref, idx, send, recv, s, t):
        return pltpu.make_async_remote_copy(src_ref=ref.at[idx], dst_ref=ref.at[idx], send_sem=send, recv_sem=recv,
                                            device_id={"sp": s, "tp": t}, device_id_type=MESH)

    def pair(ref, lo, n, send, recv, sl):
        return remote(ref, (pl.ds(lo, n), sl), send, recv, sp, other)

    def halo(ref, up, rel, send, recv):
        src_row, dst_row, dev = (rows, 0, nxt) if up == 0 else (1, rows + 1, prv)
        return pltpu.make_async_remote_copy(
            src_ref=ref.at[src_row, mine], dst_ref=ref.at[dst_row, mine], send_sem=send.at[up, rel], recv_sem=recv.at[up, rel],
            device_id={"sp": dev, "tp": tp if rel == 0 else other}, device_id_type=MESH)

    def halo_wait(ref, up, rel, send, recv):
        dst_row, dev = (0, prv) if up == 0 else (rows + 1, nxt)
        sl = mine if rel == 0 else theirs
        pltpu.make_async_remote_copy(
            src_ref=ref.at[dst_row, sl], dst_ref=ref.at[dst_row, sl], send_sem=send.at[up, rel], recv_sem=recv.at[up, rel],
            device_id={"sp": dev, "tp": tp if rel == 0 else other}, device_id_type=MESH).wait_recv()

    def halo_finish(ref, send, recv):
        for up in range(2):
            for rel in range(2):
                halo_wait(ref, up, rel, send, recv)

        @pl.when(sp == 0)
        def _():
            ref[0] = jnp.zeros((64, 1024), BF16)

        @pl.when(sp == row_devs - 1)
        def _():
            ref[rows + 1] = jnp.zeros((64, 1024), BF16)

    first = True
    for c in order:
        load(0, c).wait()
        pack(raw_g, g_all, c * chunk, 1, mine)
        if first:
            pl.semaphore_wait(barrier, len(targets))
            first = False
        if c == 0:
            for rel in range(2):
                halo(g_all, 1, rel, gh_send, gh_recv).start()
        if c == n_chunks - 1:
            for rel in range(2):
                halo(g_all, 0, rel, gh_send, gh_recv).start()
        pair(g_all, c * chunk + 1, chunk, gx_send.at[c], gx_recv.at[c], mine).start()

    for c in order:
        load(1, c).wait()
        pack(raw_a, a_pk, c * chunk, 0, slice(None))
    bacc[...] = jnp.zeros_like(bacc)
    acc[...] = jnp.zeros_like(acc)
    for c in order:
        pair(g_all, c * chunk + 1, chunk, gx_send.at[c], gx_recv.at[c], theirs).wait_recv()
    halo_finish(g_all, gh_send, gh_recv)

    def conv_tile(src, wm, b, q):
        tile = src[pl.ds(2 * b, 4), :, pl.ds(q * 256, 256)].reshape(256, 256)
        d = jnp.dot(wm[...], tile, preferred_element_type=F32)
        outs = []
        for s in range(2):
            part = d[:, s * 128:(s + 1) * 128]
            outs.append(part[64:128] + pltpu.roll(part[0:64], 127, 1) + pltpu.roll(part[128:192], 1, 1))
        return outs

    def dz_block(b):
        for q in range(4):
            for s, o in enumerate(conv_tile(g_all, wm_two, b, q)):
                lanes = pl.ds(q * 256 + s * 128, 128)
                av = a_pk[pl.ds(2 * b, 2), :, lanes].reshape(64, 128).astype(F32)
                m = jnp.where(av > 0, o, 0.0)
                bacc[...] += m
                z = m.astype(BF16)
                z_all[2 * b + 1, mine, lanes] = z[0:32]
                z_all[2 * b + 2, mine, lanes] = z[32:64]

    groups = [(0, 1), (n_blocks - 1, 1)]
    inner = n_blocks - 2
    lo = 1
    for i in range(4):
        n = inner // 4 + (1 if i < inner % 4 else 0)
        if n:
            groups.append((lo, n))
            lo += n
    for gi, (lo, n) in enumerate(groups):
        if n == 1:
            dz_block(lo)
        else:
            lax.fori_loop(lo, lo + n, lambda b, _: (dz_block(b), 0)[1], 0)
        if lo == 0:
            for rel in range(2):
                halo(z_all, 1, rel, zh_send, zh_recv).start()
        if lo + n == n_blocks:
            for rel in range(2):
                halo(z_all, 0, rel, zh_send, zh_recv).start()
        pair(z_all, 2 * lo + 1, 2 * n, zx_send.at[gi], zx_recv.at[gi], mine).start()

    def wgrad(src, gref):
        def step(b, carry):
            cur = src[pl.ds(2 * b, 2)].reshape(64, 1024)
            tiles = [cur[:, j * 128:(j + 1) * 128] for j in range(8)]
            left = jnp.concatenate([pltpu.roll(t, 1, 1) for t in tiles], axis=1)
            right = jnp.concatenate([pltpu.roll(t, 127, 1) for t in tiles], axis=1)
            lhs = jnp.concatenate([left, cur, right], axis=0)
            rhs = gref[pl.ds(2 * b, 4)].reshape(256, 1024)
            acc[...] += lax.dot_general(lhs, rhs, (((1,), (1,)), ((), ())), preferred_element_type=F32)
            return carry
        lax.fori_loop(0, n_blocks, step, 0)

    def reduce_copy(i, p, t, k, slot):
        axis = (p + t) % 3
        ref = red.at[i, p, t, slot]
        return pltpu.make_async_remote_copy(src_ref=ref, dst_ref=ref, send_sem=ar_send.at[i, p, t, k - 1], recv_sem=ar_recv.at[i, p, t, k - 1],
                                            device_id={"sp": ring_peer(axis, k), "tp": tp}, device_id_type=MESH)

    def reduce_start(i, p):
        for t in range(3):
            for k in range(1, side):
                reduce_copy(i, p, t, k, coords[(p + t) % 3]).start()

    def reduce_begin(i, extra):
        for t in range(3):
            top = acc[pl.ds(t * 64, 32), :]
            low = acc[pl.ds(t * 64 + 32, 32), :]
            e = top[:, 0:192] + low[:, 64:256]
            tail = extra if t == 0 else jnp.zeros((32, 64), F32)
            red[i, 0, t, coords[t]] = jnp.concatenate([e, tail], axis=1)
        reduce_start(i, 0)

    def reduce_step(i, p):
        for t in range(3):
            axis = (p + t) % 3
            me = coords[axis]
            for k in range(1, side):
                reduce_copy(i, p, t, k, lax.rem(me - k + side, side)).wait_recv()
            total = red[i, p, t, 0]
            for c in range(1, side):
                total = total + red[i, p, t, c]
            if p < 2:
                red[i, p + 1, t, coords[(p + 1 + t) % 3]] = total
            else:
                out = (dw_one, dw_two)[i]
                for kh in range(3):
                    out[kh, t] = total[:, (2 - kh) * 64:(3 - kh) * 64]
                if i == 0 and t == 0:
                    wide = jnp.concatenate([total[:, 192:256], jnp.zeros((32, 64), F32)], axis=1)
                    dbias[...] = jnp.sum(wide.T, axis=0, keepdims=True)
        if p < 2:
            reduce_start(i, p + 1)

    wgrad(a_pk, g_all)
    reduce_begin(1, jnp.zeros((32, 64), F32))

    for c in order:
        load(2, c).wait()
        pack(raw_x, x_pk, c * chunk, 0, slice(None))
    acc[...] = jnp.zeros_like(acc)
    for gi, (lo, n) in enumerate(groups):
        pair(z_all, 2 * lo + 1, 2 * n, zx_send.at[gi], zx_recv.at[gi], theirs).wait_recv()
    halo_finish(z_all, zh_send, zh_recv)
    wgrad(x_pk, z_all)
    both = bacc[0:32, :] + bacc[32:64, :]
    reduce_begin(0, both[:, 0:64] + both[:, 64:128])
    reduce_step(1, 0)

    def dx_block(b):
        for q in range(4):
            for s, o in enumerate(conv_tile(z_all, wm_one, b, q)):
                j = 2 * q + s
                lanes = pl.ds(j * 128, 128)
                for r in range(2):
                    gy = g_all[2 * b + 1 + r, mine, lanes].astype(F32)
                    v = (gy + o[r * 32:(r + 1) * 32]).astype(BF16)
                    raw_g[j, 2 * b + r] = v[:, 0:56]
                    raw_g[j + 8, 2 * b + r] = v[:, 64:120]

    def store(c):
        return pltpu.make_async_copy(raw_g.at[:, pl.ds(c * chunk, chunk)], dx_hbm.at[:, pl.ds(c * chunk, chunk)], out_sem.at[c])

    marks = {n_chunks // 3: ((1, 1), (0, 0)), (2 * n_chunks) // 3: ((1, 2), (0, 1))}
    for c in range(n_chunks):
        for i, p in marks.get(c, ()):
            reduce_step(i, p)
        lax.fori_loop(c * chunk // 2, (c + 1) * chunk // 2, lambda b, _: (dx_block(b), 0)[1], 0)
        store(c).start()
    reduce_step(0, 2)

    for c in range(n_chunks):
        store(c).wait()
        pair(g_all, c * chunk + 1, chunk, gx_send.at[c], gx_recv.at[c], mine).wait_send()
    for gi, (lo, n) in enumerate(groups):
        pair(z_all, 2 * lo + 1, 2 * n, zx_send.at[gi], zx_recv.at[gi], mine).wait_send()
    for up in range(2):
        for rel in range(2):
            halo(g_all, up, rel, gh_send, gh_recv).wait_send()
            halo(z_all, up, rel, zh_send, zh_recv).wait_send()
    for i in range(2):
        for p in range(3):
            for t in range(3):
                for k in range(1, side):
                    reduce_copy(i, p, t, k, coords[(p + t) % 3]).wait_send()


def solution(mesh):
    side = round(mesh.shape["sp"] ** (1 / 3))

    def local_step(x_in, act_saved, w_one, w_two, d_out):
        swap = lambda v: jnp.transpose(v, (0, 1, 3, 2))
        imgs, rows, width, ch = x_in.shape
        chunk = 8 if rows % 8 == 0 else 2
        n_chunks = rows // chunk
        raw = pltpu.VMEM((imgs, rows, ch, width), BF16)
        full = pltpu.VMEM((rows + 2, 64, 1024), BF16)
        half = pltpu.VMEM((rows, 32, 1024), BF16)
        dma = pltpu.SemaphoreType.DMA
        n_groups = 6
        vmem = pl.BlockSpec(memory_space=pltpu.VMEM)
        hbm = pl.BlockSpec(memory_space=pl.ANY)
        dx, dw_one, dw_two, dbias = pl.pallas_call(
            functools.partial(body, side, rows, chunk),
            out_shape=(
                jax.ShapeDtypeStruct((imgs, rows, ch, width), BF16),
                jax.ShapeDtypeStruct((3, 3, 32, 64), F32),
                jax.ShapeDtypeStruct((3, 3, 32, 64), F32),
                jax.ShapeDtypeStruct((1, 32), F32),
            ),
            in_specs=[hbm, hbm, hbm, vmem, vmem],
            out_specs=(hbm, vmem, vmem, vmem),
            scratch_shapes=[
                raw, raw, raw, full, full, half, half,
                pltpu.VMEM((192, 256), BF16), pltpu.VMEM((192, 256), BF16),
                pltpu.VMEM((192, 256), F32), pltpu.VMEM((64, 128), F32),
                pltpu.VMEM((2, 3, 3, side, 32, 256), F32),
                dma((3, n_chunks)), dma((n_chunks,)),
                dma((n_chunks,)), dma((n_chunks,)), dma((2, 2)), dma((2, 2)),
                dma((n_groups,)), dma((n_groups,)), dma((2, 2)), dma((2, 2)),
                dma((2, 3, 3, side - 1)), dma((2, 3, 3, side - 1)),
            ],
            compiler_params=pltpu.CompilerParams(collective_id=0, has_side_effects=True, vmem_limit_bytes=60 * 1024 * 1024),
            name="resblock_bwd",
        )(swap(x_in), swap(act_saved), swap(d_out), w_one, w_two)
        return swap(dx), dw_one, dw_two, dbias.reshape(32)

    act_spec = P("dp", "sp", None, "tp")
    kern_spec = P(None, None, "tp", None)
    grad_spec = P("dp", None, "tp", None)
    return jax.shard_map(local_step, mesh=mesh, in_specs=(act_spec, act_spec, kern_spec, kern_spec, act_spec),
                         out_specs=(act_spec, grad_spec, grad_spec, P(("dp", "tp"))), check_vma=False)
```

time: 566 us -> 73.5 us (0.13)
  blocking collectives: 178 us -> 0 us
  local copies, waits for them, and re-layouts: 128 us -> 8.76 us
  waiting for transfers between devices: 114 us -> 0 us
  matrix products: 95.7 us -> 0 us
  Pallas kernels: 0 us -> 63.9 us
  other arithmetic: 23.5 us -> 0 us
  between operations: 13.8 us -> 0.67 us
  starting transfers between devices: 10.1 us -> 0 us
    psum x1 -> x0, blocking collectives: 178 us -> none  [local_step(): grad_bias = lax.psum(jnp.sum(masked, axis=(0, 1, 2)), 'sp')]
    conv_general_dilated x4 -> x0, matrix products: 95.7 us -> none  [the longest x2 60.8 us: conv_rows(): lax.conv_general_dilated(padded, kernel[::-1, ::-1], (1, 1), ((0, 0), (1,...]
    psum x1 -> x0, waiting for transfers between devices: 79.4 us -> none  [local_step(): grad_one = lax.psum(weight_grad(dz_pad, x_in), 'sp')]
    pallas_call x0 -> x1, Pallas kernels: none -> 63.9 us  [local_step(): pl.pallas_call(functools.partial(body, side, rows, chunk), out_shape=(jax...]
    unnamed x13 -> x10, local copies, waits for them, and re-layouts: 64.1 us -> 8.76 us
    all_gather x2 -> x0, local copies, waits for them, and re-layouts: 44.2 us -> none  [the longest x1 22.1 us: local_step(): dy_pad = lax.all_gather(with_halo(d_out), 'tp', axis=3, tiled=True)]
    all_gather x2 -> x0, waiting for transfers between devices: 20.9 us -> none  [the longest x1 20.9 us: local_step(): dy_pad = lax.all_gather(with_halo(d_out), 'tp', axis=3, tiled=True)]
    concatenate x1 -> x0, local copies, waits for them, and re-layouts: 18.6 us -> none  [with_halo(): return jnp.concatenate([above, tile, below], axis=1)]
  transfers between devices with their start and end apart: 7 -> 0, of which waited for: 6 -> 0; matrix products, arithmetic and copies ran while one was open for 20% -> 0% of each run, Pallas kernels for 0% -> 0%
where the time goes in v1:
time: 73.5 us; the launch traced here: 73.4 us
  Pallas kernels  63.9 us (87%)
  local copies, waits for them, and re-layouts  8.76 us (12%)
    pallas_call x1, Pallas kernels, local_step(): pl.pallas_call(functools.partial(body, side, rows, chunk), out_shape=(jax...  63.9 us
    unnamed x10, local copies, waits for them, and re-layouts  8.76 us

profile of v1, /device:TPU:0, one launch (start us, length us, event | category | flops | bytes accessed | tf_op | source)
XLA Modules:
  0.0 73.4 jit_solution(2292772908157282848)
XLA Ops:
  0.6 63.9 %resblock_bwd.1 = (bf16[16,48,32,56]{3,2,1,0:T(8,128)(2,1)}, f32[3,3,32,64]{3,2,1,0:T(8,128)}, f32[3,3,32,64]{3,2,1,0:T(8,128)}, f32[1,32]{1,0:T(1,128)}) custom-call(bf16[16,48,32,56]{3,2,1,0:T(8,128)(2,1)} %bitcast.6, bf16[16,48,32,56]{3,2,1,0:T(8,128)(2,1)} %bitcast.7, bf16[16,48,32,56]{3,2,1,0:T(8,128)(2,1)} %bitcast.8, bf16[3,3,32,64]{3,2,1,0:T(8,128)(2,1)} %w_one.1, ...), custom_call_target="tpu_custom_call" | custom-call | tf_op jit(solution)/shard_map/resblock_bwd/pallas_call | solution.py:294
  64.6 0.0 copy-start.1
  64.6 0.0 copy-start
  64.6 0.0 copy-start.2
  64.6 6.9 %copy.13 = bf16[16,48,56,32]{2,3,1,0:T(8,128)(2,1)} copy(bf16[16,48,56,32]{2,3,1,0:T(8,128)(2,1)} %bitcast.5) | data formatting | bytes 5505024
  71.5 0.0 copy-done.1
  71.5 0.7 copy.14
  72.2 0.0 copy-done
  72.2 0.7 copy.15
  72.9 0.0 copy-done.2
  72.9 0.5 copy.16
Async XLA Ops:
  64.6 6.9 %copy-start.1 = (f32[3,3,32,64]{3,2,1,0:T(8,128)S(1)}, f32[3,3,32,64]{3,2,1,0:T(8,128)}, u32[]{:S(2)}) copy-start(f32[3,3,32,64]{3,2,1,0:T(8,128)} %get-tuple-element.17) | copy-start | bytes 221188
  64.6 7.6 %copy-start = (f32[3,3,32,64]{3,2,1,0:T(8,128)S(1)}, f32[3,3,32,64]{3,2,1,0:T(8,128)}, u32[]{:S(2)}) copy-start(f32[3,3,32,64]{3,2,1,0:T(8,128)} %get-tuple-element.18) | copy-start | bytes 221188
  64.6 8.3 %copy-start.2 = (f32[1,32]{1,0:T(1,128)S(1)}, f32[1,32]{1,0:T(1,128)}, u32[]{:S(2)}) copy-start(f32[1,32]{1,0:T(1,128)} %get-tuple-element.11) | copy-start | bytes 388

commit v2 on v1

v2 whole, which is shorter than its diff:
```python
import functools

import jax
import jax.numpy as jnp
from jax import lax
from jax.experimental import pallas as pl
from jax.experimental.pallas import tpu as pltpu
from jax.sharding import PartitionSpec as P

MESH = pl.DeviceIdType.MESH
BF16 = jnp.bfloat16
F32 = jnp.float32


def body(side, rows, x_hbm, a_hbm, g_hbm, w_one, w_two, dx_hbm, dw_one, dw_two, dbias,
         raw_g, raw_a, raw_x, g_all, z_all, wm_one, wm_two, acc, bacc, red,
         g_sem, a_sem, x_sem, out_sem, gx_send, gx_recv, gh_send, gh_recv, zx_send, zx_recv, zh_send, zh_recv,
         ar_send, ar_recv):
    sp = lax.axis_index("sp")
    tp = lax.axis_index("tp")
    row_devs = side * side * side
    n_groups = rows // 8
    n_blocks = rows // 2
    coords = (lax.rem(sp, side), lax.rem(lax.div(sp, side), side), lax.div(sp, side * side))
    strides = (1, side, side * side)
    nxt = lax.rem(sp + 1, row_devs)
    prv = lax.rem(sp + row_devs - 1, row_devs)
    other = 1 - tp
    mine = pl.ds(pl.multiple_of(tp * 32, 32), 32)
    theirs = pl.ds(pl.multiple_of(other * 32, 32), 32)

    def ring_peer(axis, k):
        me = coords[axis]
        return sp + (lax.rem(me + k, side) - me) * strides[axis]

    def load_g(c):
        part = pl.ds(c * 8, 8)
        return pltpu.make_async_copy(g_hbm.at[:, part], raw_g.at[:, part], g_sem.at[c])

    load_a = pltpu.make_async_copy(a_hbm, raw_a, a_sem)
    load_x = pltpu.make_async_copy(x_hbm, raw_x, x_sem)

    for i in range(n_groups):
        load_g((i + n_groups - 1) % n_groups).start()

    barrier = pltpu.get_barrier_semaphore()
    targets = [(sp, other), (nxt, tp), (nxt, other), (prv, tp), (prv, other)]
    for axis in range(3):
        for k in range(1, side):
            targets.append((ring_peer(axis, k), tp))
    for s, t in targets:
        pl.semaphore_signal(barrier, inc=1, device_id={"sp": s, "tp": t}, device_id_type=MESH)
    load_a.start()

    for w_ref, wm in ((w_two, wm_two), (w_one, wm_one)):
        for kw in range(3):
            for r in range(2):
                blocks = []
                for rr in range(4):
                    kh = r + 2 - rr
                    blocks.append(w_ref[kh, kw] if 0 <= kh < 3 else jnp.zeros((32, 64), BF16))
                wm[pl.ds(kw * 64 + r * 32, 32), :] = jnp.concatenate(blocks, axis=1)
    bacc[...] = jnp.zeros_like(bacc)
    acc[...] = jnp.zeros_like(acc)

    def packed(raw, h, j):
        gap = jnp.zeros((32, 8), BF16)
        return jnp.concatenate([raw[j, h], gap, raw[j + 8, h], gap], axis=1)

    def remote(ref, lo, n, sl, send, recv):
        part = ref.at[pl.ds(lo, n), :, sl]
        return pltpu.make_async_remote_copy(src_ref=part, dst_ref=part, send_sem=send, recv_sem=recv,
                                            device_id={"sp": sp, "tp": other}, device_id_type=MESH)

    def halo(ref, up, rel, send, recv):
        src_row, dst_row, dev = (rows, 0, nxt) if up == 0 else (1, rows + 1, prv)
        return pltpu.make_async_remote_copy(
            src_ref=ref.at[src_row, :, mine], dst_ref=ref.at[dst_row, :, mine], send_sem=send.at[up, rel], recv_sem=recv.at[up, rel],
            device_id={"sp": dev, "tp": tp if rel == 0 else other}, device_id_type=MESH)

    def halo_finish(ref, send, recv):
        for up in range(2):
            for rel in range(2):
                dst_row, dev = (0, prv) if up == 0 else (rows + 1, nxt)
                part = ref.at[dst_row, :, mine if rel == 0 else theirs]
                pltpu.make_async_remote_copy(
                    src_ref=part, dst_ref=part, send_sem=send.at[up, rel], recv_sem=recv.at[up, rel],
                    device_id={"sp": dev, "tp": tp if rel == 0 else other}, device_id_type=MESH).wait_recv()

        @pl.when(sp == 0)
        def _():
            ref[0] = jnp.zeros((8, 64, 128), BF16)

        @pl.when(sp == row_devs - 1)
        def _():
            ref[rows + 1] = jnp.zeros((8, 64, 128), BF16)

    def g_pair(c, sl):
        return remote(g_all, c * 8 + 1, 8, sl, gx_send.at[c], gx_recv.at[c])

    def z_pair(g, part, sl):
        lo = lax.rem(8 * g + part * 4 + rows - 4, rows) + 1
        return remote(z_all, lo, 4, sl, zx_send.at[g, part], zx_recv.at[g, part])

    pl.semaphore_wait(barrier, len(targets))

    def pack_g(i, carry):
        c = lax.rem(i + n_groups - 1, n_groups)
        load_g(c).wait()
        for h in range(8):
            for j in range(8):
                g_all[c * 8 + h + 1, j, mine] = packed(raw_g, c * 8 + h, j)

        @pl.when(i == 0)
        def _():
            for rel in range(2):
                halo(g_all, 0, rel, gh_send, gh_recv).start()

        @pl.when(i == 1)
        def _():
            for rel in range(2):
                halo(g_all, 1, rel, gh_send, gh_recv).start()

        g_pair(c, mine).start()
        return carry

    lax.fori_loop(0, n_groups, pack_g, 0)
    load_x.start()

    def conv_tile(src, wm, b, q):
        tile = jnp.concatenate([src[pl.ds(2 * b, 4), 2 * q + s].reshape(256, 128) for s in range(2)], axis=1)
        d = jnp.dot(wm[...], tile, preferred_element_type=F32)
        outs = []
        for s in range(2):
            part = d[:, s * 128:(s + 1) * 128]
            outs.append(part[64:128] + pltpu.roll(part[0:64], 127, 1) + pltpu.roll(part[128:192], 1, 1))
        return outs

    def shifted(tiles):
        left = jnp.concatenate([pltpu.roll(t, 1, 1) for t in tiles], axis=1)
        right = jnp.concatenate([pltpu.roll(t, 127, 1) for t in tiles], axis=1)
        return jnp.concatenate([left, jnp.concatenate(tiles, axis=1), right], axis=0)

    def kgrad(tiles, gref, b):
        rhs = jnp.concatenate([gref[pl.ds(2 * b, 4), j].reshape(256, 128) for j in range(8)], axis=1)
        return lax.dot_general(shifted(tiles), rhs, (((1,), (1,)), ((), ())), preferred_element_type=F32)

    def group_blocks(g):
        return [lax.rem(4 * g + k + n_blocks - 2, n_blocks) for k in range(4)]

    def middle(i, carry):
        @pl.when(i < n_groups - 1)
        def _():
            g_pair(i, theirs).wait_recv()

        bsum = None
        dw = None
        for b in group_blocks(i):
            tiles = [jnp.concatenate([packed(raw_a, 2 * b + r, j) for r in range(2)], axis=0) for j in range(8)]
            for q in range(4):
                for s, o in enumerate(conv_tile(g_all, wm_two, b, q)):
                    j = 2 * q + s
                    m = jnp.where(tiles[j].astype(F32) > 0, o, 0.0)
                    bsum = m if bsum is None else bsum + m
                    z = m.astype(BF16)
                    for r in range(2):
                        z_all[2 * b + 1 + r, j, mine] = z[r * 32:(r + 1) * 32]
            part = kgrad(tiles, g_all, b)
            dw = part if dw is None else dw + part
        bacc[...] += bsum
        acc[...] += dw

        @pl.when(i == 0)
        def _():
            for up in range(2):
                for rel in range(2):
                    halo(z_all, up, rel, zh_send, zh_recv).start()

        for part in range(2):
            z_pair(i, part, mine).start()
        return carry

    g_pair(n_groups - 1, theirs).wait_recv()
    halo_finish(g_all, gh_send, gh_recv)
    load_a.wait()
    lax.fori_loop(0, n_groups, middle, 0)

    def reduce_copy(i, p, t, k, slot):
        axis = (p + t) % 3
        ref = red.at[i, p, t, slot]
        return pltpu.make_async_remote_copy(src_ref=ref, dst_ref=ref, send_sem=ar_send.at[i, p, t, k - 1], recv_sem=ar_recv.at[i, p, t, k - 1],
                                            device_id={"sp": ring_peer(axis, k), "tp": tp}, device_id_type=MESH)

    def reduce_start(i, p):
        for t in range(3):
            for k in range(1, side):
                reduce_copy(i, p, t, k, coords[(p + t) % 3]).start()

    def reduce_begin(i, extra):
        for t in range(3):
            top = acc[pl.ds(t * 64, 32), :]
            low = acc[pl.ds(t * 64 + 32, 32), :]
            e = top[:, 0:192] + low[:, 64:256]
            tail = extra if t == 0 else jnp.zeros((32, 64), F32)
            red[i, 0, t, coords[t]] = jnp.concatenate([e, tail], axis=1)
        reduce_start(i, 0)

    def reduce_step(i, p):
        for t in range(3):
            axis = (p + t) % 3
            me = coords[axis]
            for k in range(1, side):
                reduce_copy(i, p, t, k, lax.rem(me - k + side, side)).wait_recv()
            total = red[i, p, t, 0]
            for c in range(1, side):
                total = total + red[i, p, t, c]
            if p < 2:
                red[i, p + 1, t, coords[(p + 1 + t) % 3]] = total
            else:
                out = (dw_one, dw_two)[i]
                for kh in range(3):
                    out[kh, t] = total[:, (2 - kh) * 64:(3 - kh) * 64]
                if i == 0 and t == 0:
                    wide = jnp.concatenate([total[:, 192:256], jnp.zeros((32, 64), F32)], axis=1)
                    dbias[...] = jnp.sum(wide.T, axis=0, keepdims=True)
        if p < 2:
            reduce_start(i, p + 1)

    reduce_begin(1, jnp.zeros((32, 64), F32))
    acc[...] = jnp.zeros_like(acc)

    def tail_grad(i, carry):
        @pl.when(i < n_groups - 2)
        def _():
            for part in range(2):
                z_pair(i + 2, part, theirs).wait_recv()

        dw = None
        for b in group_blocks(lax.rem(i + 1, n_groups)):
            tiles = [jnp.concatenate([packed(raw_x, 2 * b + r, j) for r in range(2)], axis=0) for j in range(8)]
            part = kgrad(tiles, z_all, b)
            dw = part if dw is None else dw + part
        acc[...] += dw
        return carry

    load_x.wait()
    for g in range(2):
        for part in range(2):
            z_pair(g, part, theirs).wait_recv()
    halo_finish(z_all, zh_send, zh_recv)
    lax.fori_loop(0, n_groups, tail_grad, 0)
    both = bacc[0:32, :] + bacc[32:64, :]
    reduce_begin(0, both[:, 0:64] + both[:, 64:128])
    reduce_step(1, 0)

    def store(c):
        part = pl.ds(c * 8, 8)
        return pltpu.make_async_copy(raw_g.at[:, part], dx_hbm.at[:, part], out_sem.at[c])

    def last(c, carry):
        for k in range(4):
            b = 4 * c + k
            for q in range(4):
                for s, o in enumerate(conv_tile(z_all, wm_one, b, q)):
                    j = 2 * q + s
                    for r in range(2):
                        gy = g_all[2 * b + 1 + r, j, mine].astype(F32)
                        v = (gy + o[r * 32:(r + 1) * 32]).astype(BF16)
                        raw_g[j, 2 * b + r] = v[:, 0:56]
                        raw_g[j + 8, 2 * b + r] = v[:, 64:120]
        store(c).start()
        return carry

    third = max(n_groups // 3, 1)
    lax.fori_loop(0, third, last, 0)
    reduce_step(1, 1)
    reduce_step(0, 0)
    lax.fori_loop(third, min(2 * third, n_groups), last, 0)
    reduce_step(1, 2)
    reduce_step(0, 1)
    lax.fori_loop(min(2 * third, n_groups), n_groups, last, 0)
    reduce_step(0, 2)

    for c in range(n_groups):
        store(c).wait()
        g_pair(c, mine).wait_send()
        for part in range(2):
            z_pair(c, part, mine).wait_send()
    for up in range(2):
        for rel in range(2):
            halo(g_all, up, rel, gh_send, gh_recv).wait_send()
            halo(z_all, up, rel, zh_send, zh_recv).wait_send()
    for i in range(2):
        for p in range(3):
            for t in range(3):
                for k in range(1, side):
                    reduce_copy(i, p, t, k, coords[(p + t) % 3]).wait_send()


def solution(mesh):
    side = round(mesh.shape["sp"] ** (1 / 3))

    def local_step(x_in, act_saved, w_one, w_two, d_out):
        swap = lambda v: jnp.transpose(v, (0, 1, 3, 2))
        imgs, rows, width, ch = x_in.shape
        n_groups = rows // 8
        raw = pltpu.VMEM((imgs, rows, ch, width), BF16)
        full = pltpu.VMEM((rows + 2, 8, 64, 128), BF16)
        dma = pltpu.SemaphoreType.DMA
        vmem = pl.BlockSpec(memory_space=pltpu.VMEM)
        hbm = pl.BlockSpec(memory_space=pl.ANY)
        dx, dw_one, dw_two, dbias = pl.pallas_call(
            functools.partial(body, side, rows),
            out_shape=(
                jax.ShapeDtypeStruct((imgs, rows, ch, width), BF16),
                jax.ShapeDtypeStruct((3, 3, 32, 64), F32),
                jax.ShapeDtypeStruct((3, 3, 32, 64), F32),
                jax.ShapeDtypeStruct((1, 32), F32),
            ),
            in_specs=[hbm, hbm, hbm, vmem, vmem],
            out_specs=(hbm, vmem, vmem, vmem),
            scratch_shapes=[
                raw, raw, raw, full, full,
                pltpu.VMEM((192, 256), BF16), pltpu.VMEM((192, 256), BF16),
                pltpu.VMEM((192, 256), F32), pltpu.VMEM((64, 128), F32),
                pltpu.VMEM((2, 3, 3, side, 32, 256), F32),
                dma((n_groups,)), dma, dma, dma((n_groups,)),
                dma((n_groups,)), dma((n_groups,)), dma((2, 2)), dma((2, 2)),
                dma((n_groups, 2)), dma((n_groups, 2)), dma((2, 2)), dma((2, 2)),
                dma((2, 3, 3, side - 1)), dma((2, 3, 3, side - 1)),
            ],
            compiler_params=pltpu.CompilerParams(collective_id=0, has_side_effects=True, vmem_limit_bytes=60 * 1024 * 1024),
            name="resblock_bwd",
        )(swap(x_in), swap(act_saved), swap(d_out), w_one, w_two)
        return swap(dx), dw_one, dw_two, dbias.reshape(32)

    act_spec = P("dp", "sp", None, "tp")
    kern_spec = P(None, None, "tp", None)
    grad_spec = P("dp", None, "tp", None)
    return jax.shard_map(local_step, mesh=mesh, in_specs=(act_spec, act_spec, kern_spec, kern_spec, act_spec),
                         out_specs=(act_spec, grad_spec, grad_spec, P(("dp", "tp"))), check_vma=False)
```

time: 73.5 us -> 59.9 us (0.81)
  Pallas kernels: 63.9 us -> 50.1 us
    pallas_call x1, Pallas kernels: 63.9 us -> 50.1 us  [local_step(): pl.pallas_call(functools.partial(body, side, rows), out_shape=(jax.ShapeD...]
where the time goes in v2:
time: 59.9 us; the launch traced here: 59.6 us
  Pallas kernels  50.1 us (84%)
  local copies, waits for them, and re-layouts  8.76 us (15%)
  between operations  0.67 us (1%)
    pallas_call x1, Pallas kernels, local_step(): pl.pallas_call(functools.partial(body, side, rows), out_shape=(jax.ShapeD...  50.1 us
    unnamed x10, local copies, waits for them, and re-layouts  8.76 us

profile of v2, /device:TPU:0, one launch (start us, length us, event | category | flops | bytes accessed | tf_op | source)
XLA Modules:
  0.0 59.6 jit_solution(9226410230296081590)
XLA Ops:
  0.6 50.1 %resblock_bwd.1 = (bf16[16,48,32,56]{3,2,1,0:T(8,128)(2,1)}, f32[3,3,32,64]{3,2,1,0:T(8,128)}, f32[3,3,32,64]{3,2,1,0:T(8,128)}, f32[1,32]{1,0:T(1,128)}) custom-call(bf16[16,48,32,56]{3,2,1,0:T(8,128)(2,1)} %bitcast.6, bf16[16,48,32,56]{3,2,1,0:T(8,128)(2,1)} %bitcast.7, bf16[16,48,32,56]{3,2,1,0:T(8,128)(2,1)} %bitcast.8, bf16[3,3,32,64]{3,2,1,0:T(8,128)(2,1)} %w_one.1, ...), custom_call_target="tpu_custom_call" | custom-call | tf_op jit(solution)/shard_map/resblock_bwd/pallas_call | solution.py:312
  50.8 0.0 copy-start.1
  50.8 0.0 copy-start
  50.8 0.0 copy-start.2
  50.8 6.9 %copy.13 = bf16[16,48,56,32]{2,3,1,0:T(8,128)(2,1)} copy(bf16[16,48,56,32]{2,3,1,0:T(8,128)(2,1)} %bitcast.5) | data formatting | bytes 5505024
  57.7 0.0 copy-done.1
  57.7 0.7 %copy.14 = f32[3,3,32,64]{3,2,1,0:T(8,128)} copy(f32[3,3,32,64]{3,2,1,0:T(8,128)S(1)} %copy-done.1) | data formatting | bytes 147456
  58.4 0.0 copy-done
  58.4 0.7 %copy.15 = f32[3,3,32,64]{3,2,1,0:T(8,128)} copy(f32[3,3,32,64]{3,2,1,0:T(8,128)S(1)} %copy-done) | data formatting | bytes 147456
  59.1 0.0 copy-done.2
  59.1 0.5 copy.16
Async XLA Ops:
  50.8 6.9 %copy-start.1 = (f32[3,3,32,64]{3,2,1,0:T(8,128)S(1)}, f32[3,3,32,64]{3,2,1,0:T(8,128)}, u32[]{:S(2)}) copy-start(f32[3,3,32,64]{3,2,1,0:T(8,128)} %get-tuple-element.17) | copy-start | bytes 221188
  50.8 7.6 %copy-start = (f32[3,3,32,64]{3,2,1,0:T(8,128)S(1)}, f32[3,3,32,64]{3,2,1,0:T(8,128)}, u32[]{:S(2)}) copy-start(f32[3,3,32,64]{3,2,1,0:T(8,128)} %get-tuple-element.18) | copy-start | bytes 221188
  50.8 8.3 %copy-start.2 = (f32[1,32]{1,0:T(1,128)S(1)}, f32[1,32]{1,0:T(1,128)}, u32[]{:S(2)}) copy-start(f32[1,32]{1,0:T(1,128)} %get-tuple-element.11) | copy-start | bytes 388

commit v3 on v2

--- a/solution.py
+++ b/solution.py
@@ -253,10 +253,6 @@
     reduce_begin(0, both[:, 0:64] + both[:, 64:128])
     reduce_step(1, 0)
 
-    def store(c):
-        part = pl.ds(c * 8, 8)
-        return pltpu.make_async_copy(raw_g.at[:, part], dx_hbm.at[:, part], out_sem.at[c])
-
     def last(c, carry):
         for k in range(4):
             b = 4 * c + k
@@ -266,9 +262,8 @@
                     for r in range(2):
                         gy = g_all[2 * b + 1 + r, j, mine].astype(F32)
                         v = (gy + o[r * 32:(r + 1) * 32]).astype(BF16)
-                        raw_g[j, 2 * b + r] = v[:, 0:56]
-                        raw_g[j + 8, 2 * b + r] = v[:, 64:120]
-        store(c).start()
+                        dx_hbm[j, 2 * b + r] = v[:, 0:56]
+                        dx_hbm[j + 8, 2 * b + r] = v[:, 64:120]
         return carry
 
     third = max(n_groups // 3, 1)
@@ -282,7 +277,6 @@
     reduce_step(0, 2)
 
     for c in range(n_groups):
-        store(c).wait()
         g_pair(c, mine).wait_send()
         for part in range(2):
             z_pair(c, part, mine).wait_send()
@@ -312,13 +306,13 @@
         dx, dw_one, dw_two, dbias = pl.pallas_call(
             functools.partial(body, side, rows),
             out_shape=(
-                jax.ShapeDtypeStruct((imgs, rows, ch, width), BF16),
-                jax.ShapeDtypeStruct((3, 3, 32, 64), F32),
-                jax.ShapeDtypeStruct((3, 3, 32, 64), F32),
-                jax.ShapeDtypeStruct((1, 32), F32),
+                pltpu.VMEM((imgs, rows, ch, width), BF16),
+                pltpu.VMEM((3, 3, 32, 64), F32),
+                pltpu.VMEM((3, 3, 32, 64), F32),
+                pltpu.VMEM((1, 32), F32),
             ),
             in_specs=[hbm, hbm, hbm, vmem, vmem],
-            out_specs=(hbm, vmem, vmem, vmem),
+            out_specs=(vmem, vmem, vmem, vmem),
             scratch_shapes=[
                 raw, raw, raw, full, full,
                 pltpu.VMEM((192, 256), BF16), pltpu.VMEM((192, 256), BF16),
@@ -329,7 +323,7 @@
                 dma((n_groups, 2)), dma((n_groups, 2)), dma((2, 2)), dma((2, 2)),
                 dma((2, 3, 3, side - 1)), dma((2, 3, 3, side - 1)),
             ],
-            compiler_params=pltpu.CompilerParams(collective_id=0, has_side_effects=True, vmem_limit_bytes=60 * 1024 * 1024),
+            compiler_params=pltpu.CompilerParams(collective_id=0, has_side_effects=True, vmem_limit_bytes=46 * 1024 * 1024),
             name="resblock_bwd",
         )(swap(x_in), swap(act_saved), swap(d_out), w_one, w_two)
         return swap(dx), dw_one, dw_two, dbias.reshape(32)

time: 59.9 us -> 55.8 us (0.932)
  local copies, waits for them, and re-layouts: 8.76 us -> 6.3 us
  Pallas kernels: 50.1 us -> 48.2 us
    unnamed x10 -> x8, local copies, waits for them, and re-layouts: 8.76 us -> 6.3 us
    pallas_call x1, Pallas kernels: 50.1 us -> 48.2 us  [local_step(): pl.pallas_call(functools.partial(body, side, rows), out_shape=(pltpu.VMEM...]
where the time goes in v3:
time: 55.8 us; the launch traced here: 55.1 us
  Pallas kernels  48.2 us (86%)
  local copies, waits for them, and re-layouts  6.3 us (11%)
  between operations  0.65 us (1%)
    pallas_call x1, Pallas kernels, local_step(): pl.pallas_call(functools.partial(body, side, rows), out_shape=(pltpu.VMEM...  48.2 us
    unnamed x8, local copies, waits for them, and re-layouts  6.3 us

profile of v3, /device:TPU:0, one launch (start us, length us, event | category | flops | bytes accessed | tf_op | source)
XLA Modules:
  0.0 55.1 jit_solution(3695852410170207781)
XLA Ops:
  0.6 0.0 copy-start
  0.6 0.9 %copy-done = bf16[3,3,32,64]{3,2,1,0:T(8,128)(2,1)S(1)} copy-done((bf16[3,3,32,64]{3,2,1,0:T(8,128)(2,1)S(1)}, bf16[3,3,32,64]{3,2,1,0:T(8,128)(2,1)}, u32[]{:S(2)}) %copy-start) | copy-done | bytes 36888
  1.5 0.0 copy-start.1
  1.5 0.9 %copy-done.1 = bf16[3,3,32,64]{3,2,1,0:T(8,128)(2,1)S(1)} copy-done((bf16[3,3,32,64]{3,2,1,0:T(8,128)(2,1)S(1)}, bf16[3,3,32,64]{3,2,1,0:T(8,128)(2,1)}, u32[]{:S(2)}) %copy-start.1) | copy-done | bytes 36888
  2.4 48.2 %resblock_bwd.1 = (bf16[16,48,32,56]{3,2,1,0:T(8,128)(2,1)S(1)}, f32[3,3,32,64]{3,2,1,0:T(8,128)S(1)}, f32[3,3,32,64]{3,2,1,0:T(8,128)S(1)}, f32[1,32]{1,0:T(1,128)S(1)}) custom-call(bf16[16,48,32,56]{3,2,1,0:T(8,128)(2,1)} %bitcast.7, bf16[16,48,32,56]{3,2,1,0:T(8,128)(2,1)} %bitcast.8, bf16[16,48,32,56]{3,2,1,0:T(8,128)(2,1)} %bitcast.9, ...), custom_call_target="tpu_custom_call" | custom-call | tf_op jit(solution)/shard_map/resblock_bwd/pallas_call | solution.py:306
  50.6 2.7 %copy.13 = bf16[16,48,56,32]{2,3,1,0:T(8,128)(2,1)} copy(bf16[16,48,56,32]{2,3,1,0:T(8,128)(2,1)S(1)} %bitcast.5) | data formatting | bytes 5505024
  53.3 0.5 copy.16
  53.8 0.7 %copy.14 = f32[3,3,32,64]{3,2,1,0:T(8,128)} copy(f32[3,3,32,64]{3,2,1,0:T(8,128)S(1)} %get-tuple-element.13) | data formatting | bytes 147456
  54.4 0.7 %copy.15 = f32[3,3,32,64]{3,2,1,0:T(8,128)} copy(f32[3,3,32,64]{3,2,1,0:T(8,128)S(1)} %get-tuple-element.14) | data formatting | bytes 147456
Async XLA Ops:
  0.6 0.9 %copy-start = (bf16[3,3,32,64]{3,2,1,0:T(8,128)(2,1)S(1)}, bf16[3,3,32,64]{3,2,1,0:T(8,128)(2,1)}, u32[]{:S(2)}) copy-start(bf16[3,3,32,64]{3,2,1,0:T(8,128)(2,1)} %w_one.1) | copy-start | bytes 110596
  1.5 0.9 %copy-start.1 = (bf16[3,3,32,64]{3,2,1,0:T(8,128)(2,1)S(1)}, bf16[3,3,32,64]{3,2,1,0:T(8,128)(2,1)}, u32[]{:S(2)}) copy-start(bf16[3,3,32,64]{3,2,1,0:T(8,128)(2,1)} %w_two.1) | copy-start | bytes 110596

commit v4 on v3

--- a/solution.py
+++ b/solution.py
@@ -13,8 +13,8 @@
 
 
 def body(side, rows, x_hbm, a_hbm, g_hbm, w_one, w_two, dx_hbm, dw_one, dw_two, dbias,
-         raw_g, raw_a, raw_x, g_all, z_all, wm_one, wm_two, acc, bacc, red,
-         g_sem, a_sem, x_sem, out_sem, gx_send, gx_recv, gh_send, gh_recv, zx_send, zx_recv, zh_send, zh_recv,
+         raw_g, raw_a, raw_x, g_all, z_all, w_raw, wm_one, wm_two, acc, bacc, red,
+         g_sem, a_sem, x_sem, w_sem, gx_send, gx_recv, gh_send, gh_recv, zx_send, zx_recv, zh_send, zh_recv,
          ar_send, ar_recv):
     sp = lax.axis_index("sp")
     tp = lax.axis_index("tp")
@@ -33,15 +33,25 @@
         me = coords[axis]
         return sp + (lax.rem(me + k, side) - me) * strides[axis]
 
+    def load(hbm, raw, sem, c):
+        part = pl.ds(c * 8, 8)
+        return pltpu.make_async_copy(hbm.at[:, part], raw.at[:, part], sem.at[c])
+
     def load_g(c):
-        part = pl.ds(c * 8, 8)
-        return pltpu.make_async_copy(g_hbm.at[:, part], raw_g.at[:, part], g_sem.at[c])
-
-    load_a = pltpu.make_async_copy(a_hbm, raw_a, a_sem)
+        return load(g_hbm, raw_g, g_sem, c)
+
+    def load_a(c):
+        return load(a_hbm, raw_a, a_sem, c)
+
     load_x = pltpu.make_async_copy(x_hbm, raw_x, x_sem)
-
-    for i in range(n_groups):
-        load_g((i + n_groups - 1) % n_groups).start()
+    load_w = [pltpu.make_async_copy(w, w_raw.at[i], w_sem.at[i]) for i, w in enumerate((w_one, w_two))]
+
+    load_g(0).start()
+    for w in load_w:
+        w.start()
+    for c in range(1, min(3, n_groups)):
+        load_g(c).start()
+    load_a(0).start()
 
     barrier = pltpu.get_barrier_semaphore()
     targets = [(sp, other), (nxt, tp), (nxt, other), (prv, tp), (prv, other)]
@@ -50,15 +60,15 @@
             targets.append((ring_peer(axis, k), tp))
     for s, t in targets:
         pl.semaphore_signal(barrier, inc=1, device_id={"sp": s, "tp": t}, device_id_type=MESH)
-    load_a.start()
-
-    for w_ref, wm in ((w_two, wm_two), (w_one, wm_one)):
+
+    for i, wm in ((1, wm_two), (0, wm_one)):
+        load_w[i].wait()
         for kw in range(3):
             for r in range(2):
                 blocks = []
                 for rr in range(4):
                     kh = r + 2 - rr
-                    blocks.append(w_ref[kh, kw] if 0 <= kh < 3 else jnp.zeros((32, 64), BF16))
+                    blocks.append(w_raw[i, kh, kw] if 0 <= kh < 3 else jnp.zeros((32, 64), BF16))
                 wm[pl.ds(kw * 64 + r * 32, 32), :] = jnp.concatenate(blocks, axis=1)
     bacc[...] = jnp.zeros_like(bacc)
     acc[...] = jnp.zeros_like(acc)
@@ -104,27 +114,33 @@
 
     pl.semaphore_wait(barrier, len(targets))
 
-    def pack_g(i, carry):
-        c = lax.rem(i + n_groups - 1, n_groups)
-        load_g(c).wait()
+    def pack_rows(c):
         for h in range(8):
             for j in range(8):
                 g_all[c * 8 + h + 1, j, mine] = packed(raw_g, c * 8 + h, j)
 
-        @pl.when(i == 0)
-        def _():
-            for rel in range(2):
-                halo(g_all, 0, rel, gh_send, gh_recv).start()
-
-        @pl.when(i == 1)
+    def pack_g(c, carry):
+        load_g(c).wait()
+        pack_rows(c)
+
+        @pl.when(c == 0)
         def _():
             for rel in range(2):
                 halo(g_all, 1, rel, gh_send, gh_recv).start()
 
         g_pair(c, mine).start()
+
+        @pl.when(c + ahead < n_groups)
+        def _():
+            load_g(c + ahead).start()
+
+        load_a(c + 1).start()
         return carry
 
-    lax.fori_loop(0, n_groups, pack_g, 0)
+    ahead = min(3, n_groups - 1)
+    lax.fori_loop(0, ahead, pack_g, 0)
+    for c in range(ahead + 1, n_groups):
+        load_a(c).start()
     load_x.start()
 
     def conv_tile(src, wm, b, q):
@@ -148,14 +164,21 @@
     def group_blocks(g):
         return [lax.rem(4 * g + k + n_blocks - 2, n_blocks) for k in range(4)]
 
-    def middle(i, carry):
-        @pl.when(i < n_groups - 1)
-        def _():
-            g_pair(i, theirs).wait_recv()
-
+    def middle(i, ahead):
+        if ahead:
+            load_g(i + ahead).wait()
+
+        @pl.when(i + 1 < n_groups)
+        def _():
+            load_a(i + 1).wait()
+            g_pair(i + 1, theirs).wait_recv()
+
+        if ahead:
+            pack_rows(i + ahead)
+        g = lax.rem(i + 1, n_groups)
         bsum = None
         dw = None
-        for b in group_blocks(i):
+        for b in group_blocks(g):
             tiles = [jnp.concatenate([packed(raw_a, 2 * b + r, j) for r in range(2)], axis=0) for j in range(8)]
             for q in range(4):
                 for s, o in enumerate(conv_tile(g_all, wm_two, b, q)):
@@ -169,74 +192,103 @@
             dw = part if dw is None else dw + part
         bacc[...] += bsum
         acc[...] += dw
-
-        @pl.when(i == 0)
-        def _():
-            for up in range(2):
+        if ahead:
+            g_pair(i + ahead, mine).start()
+
+            @pl.when(i + ahead == n_groups - 1)
+            def _():
                 for rel in range(2):
-                    halo(z_all, up, rel, zh_send, zh_recv).start()
+                    halo(g_all, 0, rel, gh_send, gh_recv).start()
 
         for part in range(2):
-            z_pair(i, part, mine).start()
+            z_pair(g, part, mine).start()
+
+    load_a(0).wait()
+    g_pair(0, theirs).wait_recv()
+
+    def middle_pack(i, carry):
+        middle(i, ahead)
         return carry
 
-    g_pair(n_groups - 1, theirs).wait_recv()
-    halo_finish(g_all, gh_send, gh_recv)
-    load_a.wait()
-    lax.fori_loop(0, n_groups, middle, 0)
+    def middle_plain(i, carry):
+        @pl.when(i == n_groups - 1)
+        def _():
+            halo_finish(g_all, gh_send, gh_recv)
+
+        middle(i, 0)
+        return carry
+
+    lax.fori_loop(0, n_groups - ahead, middle_pack, 0)
+    lax.fori_loop(n_groups - ahead, n_groups, middle_plain, 0)
+    for up in range(2):
+        for rel in range(2):
+            halo(z_all, up, rel, zh_send, zh_recv).start()
 
     def reduce_copy(i, p, t, k, slot):
         axis = (p + t) % 3
-        ref = red.at[i, p, t, slot]
+        ref = red.at[i, p, t, slot, pl.ds(0, 56 if i == 0 and t == 0 else 48)]
         return pltpu.make_async_remote_copy(src_ref=ref, dst_ref=ref, send_sem=ar_send.at[i, p, t, k - 1], recv_sem=ar_recv.at[i, p, t, k - 1],
                                             device_id={"sp": ring_peer(axis, k), "tp": tp}, device_id_type=MESH)
 
     def reduce_start(i, p):
         for t in range(3):
-            for k in range(1, side):
+            for k in (2, 1, 3)[:side - 1] if side > 2 else (1,):
                 reduce_copy(i, p, t, k, coords[(p + t) % 3]).start()
 
-    def reduce_begin(i, extra):
+    def reduce_begin(i):
         for t in range(3):
             top = acc[pl.ds(t * 64, 32), :]
             low = acc[pl.ds(t * 64 + 32, 32), :]
             e = top[:, 0:192] + low[:, 64:256]
-            tail = extra if t == 0 else jnp.zeros((32, 64), F32)
-            red[i, 0, t, coords[t]] = jnp.concatenate([e, tail], axis=1)
+            red[i, 0, t, coords[t], pl.ds(0, 32)] = e[:, 0:128]
+            red[i, 0, t, coords[t], pl.ds(32, 16)] = jnp.concatenate([e[0:16, 128:192], e[16:32, 128:192]], axis=1)
+            if i == 0 and t == 0:
+                both = bacc[0:32, :] + bacc[32:64, :]
+                col = jnp.sum(both, axis=1, keepdims=True)
+                row = jnp.broadcast_to(col, (32, 128)).T[0:8]
+                red[i, 0, t, coords[t], pl.ds(48, 8)] = jnp.concatenate([row, jnp.zeros((8, 96), F32)], axis=1)
         reduce_start(i, 0)
 
     def reduce_step(i, p):
         for t in range(3):
+            n = 56 if i == 0 and t == 0 else 48
             axis = (p + t) % 3
             me = coords[axis]
             for k in range(1, side):
                 reduce_copy(i, p, t, k, lax.rem(me - k + side, side)).wait_recv()
-            total = red[i, p, t, 0]
+            total = red[i, p, t, 0, pl.ds(0, n)]
             for c in range(1, side):
-                total = total + red[i, p, t, c]
+                total = total + red[i, p, t, c, pl.ds(0, n)]
             if p < 2:
-                red[i, p + 1, t, coords[(p + 1 + t) % 3]] = total
+                red[i, p + 1, t, coords[(p + 1 + t) % 3], pl.ds(0, n)] = total
             else:
                 out = (dw_one, dw_two)[i]
-                for kh in range(3):
-                    out[kh, t] = total[:, (2 - kh) * 64:(3 - kh) * 64]
+                out[2, t] = total[0:32, 0:64]
+                out[1, t] = total[0:32, 64:128]
+                out[0, t] = jnp.concatenate([total[32:48, 0:64], total[32:48, 64:128]], axis=0)
                 if i == 0 and t == 0:
-                    wide = jnp.concatenate([total[:, 192:256], jnp.zeros((32, 64), F32)], axis=1)
-                    dbias[...] = jnp.sum(wide.T, axis=0, keepdims=True)
+                    dbias[...] = total[48:49, 0:32]
         if p < 2:
             reduce_start(i, p + 1)
 
-    reduce_begin(1, jnp.zeros((32, 64), F32))
+    reduce_begin(1)
     acc[...] = jnp.zeros_like(acc)
 
+    def z_wait(g):
+        for part in range(2):
+            z_pair(g, part, theirs).wait_recv()
+
     def tail_grad(i, carry):
-        @pl.when(i < n_groups - 2)
-        def _():
-            for part in range(2):
-                z_pair(i + 2, part, theirs).wait_recv()
+        @pl.when((i > 0) & (i < n_groups - 2))
+        def _():
+            z_wait(lax.rem(i + 3, n_groups))
+
+        @pl.when(i == n_groups - 2)
+        def _():
+            halo_finish(z_all, zh_send, zh_recv)
 
         dw = None
-        for b in group_blocks(lax.rem(i + 1, n_groups)):
+        for b in group_blocks(lax.rem(i + 2, n_groups)):
             tiles = [jnp.concatenate([packed(raw_x, 2 * b + r, j) for r in range(2)], axis=0) for j in range(8)]
             part = kgrad(tiles, z_all, b)
             dw = part if dw is None else dw + part
@@ -244,14 +296,12 @@
         return carry
 
     load_x.wait()
-    for g in range(2):
-        for part in range(2):
-            z_pair(g, part, theirs).wait_recv()
-    halo_finish(z_all, zh_send, zh_recv)
-    lax.fori_loop(0, n_groups, tail_grad, 0)
-    both = bacc[0:32, :] + bacc[32:64, :]
-    reduce_begin(0, both[:, 0:64] + both[:, 64:128])
+    for g in range(1, min(4, n_groups)):
+        z_wait(g)
+    lax.fori_loop(0, n_groups - 2, tail_grad, 0)
     reduce_step(1, 0)
+    lax.fori_loop(n_groups - 2, n_groups, tail_grad, 0)
+    reduce_begin(0)
 
     def last(c, carry):
         for k in range(4):
@@ -291,6 +341,15 @@
                     reduce_copy(i, p, t, k, coords[(p + t) % 3]).wait_send()
 
 
+def write_out(*refs):
+    sems = refs[8]
+    copies = [pltpu.make_async_copy(refs[i], refs[4 + i], sems.at[i]) for i in range(4)]
+    for copy in copies:
+        copy.start()
+    for copy in copies:
+        copy.wait()
+
+
 def solution(mesh):
     side = round(mesh.shape["sp"] ** (1 / 3))
 
@@ -302,7 +361,7 @@
         full = pltpu.VMEM((rows + 2, 8, 64, 128), BF16)
         dma = pltpu.SemaphoreType.DMA
         vmem = pl.BlockSpec(memory_space=pltpu.VMEM)
-        hbm = pl.BlockSpec(memory_space=pl.ANY)
+        hbm = pl.BlockSpec(memory_space=pltpu.HBM)
         dx, dw_one, dw_two, dbias = pl.pallas_call(
             functools.partial(body, side, rows),
             out_shape=(
@@ -311,21 +370,31 @@
                 pltpu.VMEM((3, 3, 32, 64), F32),
                 pltpu.VMEM((1, 32), F32),
             ),
-            in_specs=[hbm, hbm, hbm, vmem, vmem],
+            in_specs=[hbm, hbm, hbm, hbm, hbm],
             out_specs=(vmem, vmem, vmem, vmem),
             scratch_shapes=[
-                raw, raw, raw, full, full,
+                raw, raw, raw, full, full, pltpu.VMEM((2, 3, 3, 32, 64), BF16),
                 pltpu.VMEM((192, 256), BF16), pltpu.VMEM((192, 256), BF16),
                 pltpu.VMEM((192, 256), F32), pltpu.VMEM((64, 128), F32),
-                pltpu.VMEM((2, 3, 3, side, 32, 256), F32),
-                dma((n_groups,)), dma, dma, dma((n_groups,)),
+                pltpu.VMEM((2, 3, 3, side, 56, 128), F32),
+                dma((n_groups,)), dma((n_groups,)), dma, dma((2,)),
                 dma((n_groups,)), dma((n_groups,)), dma((2, 2)), dma((2, 2)),
                 dma((n_groups, 2)), dma((n_groups, 2)), dma((2, 2)), dma((2, 2)),
                 dma((2, 3, 3, side - 1)), dma((2, 3, 3, side - 1)),
             ],
             compiler_params=pltpu.CompilerParams(collective_id=0, has_side_effects=True, vmem_limit_bytes=46 * 1024 * 1024),
             name="resblock_bwd",
-        )(swap(x_in), swap(act_saved), swap(d_out), w_one, w_two)
+        )(*(pltpu.with_memory_space_constraint(v, pltpu.HBM) for v in (swap(x_in), swap(act_saved), swap(d_out), w_one, w_two)))
+        results = (dx, dw_one, dw_two, dbias)
+        dx, dw_one, dw_two, dbias = pl.pallas_call(
+            write_out,
+            out_shape=tuple(jax.ShapeDtypeStruct(v.shape, v.dtype) for v in results),
+            in_specs=[vmem] * 4,
+            out_specs=(hbm,) * 4,
+            scratch_shapes=[dma((4,))],
+            compiler_params=pltpu.CompilerParams(vmem_limit_bytes=1024 * 1024),
+            name="write_out",
+        )(*results)
         return swap(dx), dw_one, dw_two, dbias.reshape(32)
 
     act_spec = P("dp", "sp", None, "tp")

time: 55.8 us -> 50.6 us (0.907)
  local copies, waits for them, and re-layouts: 6.3 us -> 0 us
  Pallas kernels: 48.2 us -> 49.2 us
    unnamed x8 -> x0, local copies, waits for them, and re-layouts: 6.3 us -> none
    pallas_call x0 -> x1, Pallas kernels: none -> 2.82 us  [local_step(): pl.pallas_call(write_out, out_shape=tuple((jax.ShapeDtypeStruct(v.shape,...]
    pallas_call x1, Pallas kernels: 48.2 us -> 46.4 us  [local_step(): pl.pallas_call(functools.partial(body, side, rows), out_shape=(pltpu.VMEM...]
where the time goes in v4:
time: 50.6 us; the launch traced here: 49.8 us
  Pallas kernels  49.2 us (97%)
  between operations  0.64 us (1%)
    pallas_call x1, Pallas kernels, local_step(): pl.pallas_call(functools.partial(body, side, rows), out_shape=(pltpu.VMEM...  46.4 us
    pallas_call x1, Pallas kernels, local_step(): pl.pallas_call(write_out, out_shape=tuple((jax.ShapeDtypeStruct(v.shape,...  2.82 us

profile of v4, /device:TPU:0, one launch (start us, length us, event | category | flops | bytes accessed | tf_op | source)
XLA Modules:
  0.0 49.8 jit_solution(4339457847608689529)
XLA Ops:
  0.6 46.4 %resblock_bwd.1 = (bf16[16,48,32,56]{3,2,1,0:T(8,128)(2,1)S(1)}, f32[3,3,32,64]{3,2,1,0:T(8,128)S(1)}, f32[3,3,32,64]{3,2,1,0:T(8,128)S(1)}, f32[1,32]{1,0:T(1,128)S(1)}) custom-call(bf16[16,48,32,56]{3,2,1,0:T(8,128)(2,1)} %bitcast.5, bf16[16,48,32,56]{3,2,1,0:T(8,128)(2,1)} %bitcast.6, bf16[16,48,32,56]{3,2,1,0:T(8,128)(2,1)} %bitcast.7, ...), custom_call_target="tpu_custom_call" | custom-call | tf_op jit(solution)/shard_map/resblock_bwd/pallas_call | solution.py:365
  47.0 2.8 %write_out.1 = (bf16[16,48,32,56]{3,2,1,0:T(8,128)(2,1)}, f32[3,3,32,64]{3,2,1,0:T(8,128)}, f32[3,3,32,64]{3,2,1,0:T(8,128)}, f32[1,32]{1,0:T(1,128)}) custom-call(bf16[16,48,32,56]{3,2,1,0:T(8,128)(2,1)S(1)} %get-tuple-element.12.refs_0_, f32[3,3,32,64]{3,2,1,0:T(8,128)S(1)} %get-tuple-element.13.refs_1_, f32[3,3,32,64]{3,2,1,0:T(8,128)S(1)} %get-tuple-element.14.refs_2_, ...), custom_call_target="tpu_custom_call" | custom-call | tf_op jit(solution)/shard_map/write_out/pallas_call | solution.py:389

commit v5 on v4

--- a/solution.py
+++ b/solution.py
@@ -61,6 +61,136 @@
     for s, t in targets:
         pl.semaphore_signal(barrier, inc=1, device_id={"sp": s, "tp": t}, device_id_type=MESH)
 
+    bacc[...] = jnp.zeros_like(bacc)
+    acc[...] = jnp.zeros_like(acc)
+
+    def packed(raw, h, j):
+        gap = jnp.zeros((32, 8), BF16)
+        return jnp.concatenate([raw[j, h], gap, raw[j + 8, h], gap], axis=1)
+
+    def remote(ref, lo, n, sl, send, recv):
+        part = ref.at[pl.ds(lo, n), :, sl]
+        return pltpu.make_async_remote_copy(src_ref=part, dst_ref=part, send_sem=send, recv_sem=recv,
+                                            device_id={"sp": sp, "tp": other}, device_id_type=MESH)
+
+    def halo(ref, up, rel, send, recv):
+        src_row, dst_row, dev = (rows, 0, nxt) if up == 0 else (1, rows + 1, prv)
+        return pltpu.make_async_remote_copy(
+            src_ref=ref.at[src_row, :, mine], dst_ref=ref.at[dst_row, :, mine], send_sem=send.at[up, rel], recv_sem=recv.at[up, rel],
+            device_id={"sp": dev, "tp": tp if rel == 0 else other}, device_id_type=MESH)
+
+    def halo_finish(ref, send, recv):
+        for up in range(2):
+            for rel in range(2):
+                dst_row, dev = (0, prv) if up == 0 else (rows + 1, nxt)
+                part = ref.at[dst_row, :, mine if rel == 0 else theirs]
+                pltpu.make_async_remote_copy(
+                    src_ref=part, dst_ref=part, send_sem=send.at[up, rel], recv_sem=recv.at[up, rel],
+                    device_id={"sp": dev, "tp": tp if rel == 0 else other}, device_id_type=MESH).wait_recv()
+
+        @pl.when(sp == 0)
+        def _():
+            ref[0] = jnp.zeros((8, 64, 128), BF16)
+
+        @pl.when(sp == row_devs - 1)
+        def _():
+            ref[rows + 1] = jnp.zeros((8, 64, 128), BF16)
+
+    def g_pair(c, sl):
+        return remote(g_all, c * 8 + 1, 8, sl, gx_send.at[c], gx_recv.at[c])
+
+    def z_pair(g, part, sl):
+        lo = lax.rem(8 * g + part * 4 + rows - 4, rows) + 1
+        return remote(z_all, lo, 4, sl, zx_send.at[g, part], zx_recv.at[g, part])
+
+    pl.semaphore_wait(barrier, len(targets))
+
+    def pack_rows(c):
+        for h in range(8):
+            for j in range(8):
+                g_all[c * 8 + h + 1, j, mine] = packed(raw_g, c * 8 + h, j)
+
+    def pack_g(c, carry):
+        load_g(c).wait()
+        pack_rows(c)
+
+        @pl.when(c == 0)
+        def _():
+            for rel in range(2):
+                halo(g_all, 1, rel, gh_send, gh_recv).start()
+
+        g_pair(c, mine).start()
+
+        @pl.when(c + ahead < n_groups)
+        def _():
+            load_g(c + ahead).start()
+
+        load_a(c + 1).start()
+        return carry
+
+    ahead = min(3, n_groups - 1)
+    lax.fori_loop(0, ahead, pack_g, 0)
+    for c in range(ahead + 1, n_groups):
+        load_a(c).start()
+    load_x.start()
+
+    def conv_tile(src, wm, b, q):
+        tile = jnp.concatenate([src[pl.ds(2 * b, 4), 2 * q + s].reshape(256, 128) for s in range(2)], axis=1)
+        d = jnp.dot(wm[...], tile, preferred_element_type=F32)
+        outs = []
+        for s in range(2):
+            part = d[:, s * 128:(s + 1) * 128]
+            outs.append(part[64:128] + pltpu.roll(part[0:64], 127, 1) + pltpu.roll(part[128:192], 1, 1))
+        return outs
+
+    def shifted(tiles):
+        left = jnp.concatenate([pltpu.roll(t, 1, 1) for t in tiles], axis=1)
+        right = jnp.concatenate([pltpu.roll(t, 127, 1) for t in tiles], axis=1)
+        return jnp.concatenate([left, jnp.concatenate(tiles, axis=1), right], axis=0)
+
+    def kgrad(tiles, gref, b):
+        rhs = jnp.concatenate([gref[pl.ds(2 * b, 4), j].reshape(256, 128) for j in range(8)], axis=1)
+        return lax.dot_general(shifted(tiles), rhs, (((1,), (1,)), ((), ())), preferred_element_type=F32)
+
+    def group_blocks(g):
+        return [lax.rem(4 * g + k + n_blocks - 2, n_blocks) for k in range(4)]
+
+    def middle(i, ahead):
+        if ahead:
+            load_g(i + ahead).wait()
+
+        @pl.when(i + 1 < n_groups)
+        def _():
+            load_a(i + 1).wait()
+            g_pair(i + 1, theirs).wait_recv()
+
+        if ahead:
+            pack_rows(i + ahead)
+        g = lax.rem(i + 1, n_groups)
+        bsum = None
+        for slot, b in enumerate(group_blocks(g)):
+            tiles = [jnp.concatenate([packed(raw_a, 2 * b + r, j) for r in range(2)], axis=0) for j in range(8)]
+            for q in range(4):
+                for s, o in enumerate(conv_tile(g_all, wm_two, b, q)):
+                    j = 2 * q + s
+                    m = jnp.where(tiles[j].astype(F32) > 0, o, 0.0)
+                    bsum = m if bsum is None else bsum + m
+                    z = m.astype(BF16)
+                    for r in range(2):
+                        z_all[2 * b + 1 + r, j, mine] = z[r * 32:(r + 1) * 32]
+            acc[slot % 4] += kgrad(tiles, g_all, b)
+        bacc[...] += bsum
+        if ahead:
+            g_pair(i + ahead, mine).start()
+
+            @pl.when(i + ahead == n_groups - 1)
+            def _():
+                for rel in range(2):
+                    halo(g_all, 0, rel, gh_send, gh_recv).start()
+
+        for part in range(2):
+            z_pair(g, part, mine).start()
+
     for i, wm in ((1, wm_two), (0, wm_one)):
         load_w[i].wait()
         for kw in range(3):
@@ -70,139 +200,6 @@
                     kh = r + 2 - rr
                     blocks.append(w_raw[i, kh, kw] if 0 <= kh < 3 else jnp.zeros((32, 64), BF16))
                 wm[pl.ds(kw * 64 + r * 32, 32), :] = jnp.concatenate(blocks, axis=1)
-    bacc[...] = jnp.zeros_like(bacc)
-    acc[...] = jnp.zeros_like(acc)
-
-    def packed(raw, h, j):
-        gap = jnp.zeros((32, 8), BF16)
-        return jnp.concatenate([raw[j, h], gap, raw[j + 8, h], gap], axis=1)
-
-    def remote(ref, lo, n, sl, send, recv):
-        part = ref.at[pl.ds(lo, n), :, sl]
-        return pltpu.make_async_remote_copy(src_ref=part, dst_ref=part, send_sem=send, recv_sem=recv,
-                                            device_id={"sp": sp, "tp": other}, device_id_type=MESH)
-
-    def halo(ref, up, rel, send, recv):
-        src_row, dst_row, dev = (rows, 0, nxt) if up == 0 else (1, rows + 1, prv)
-        return pltpu.make_async_remote_copy(
-            src_ref=ref.at[src_row, :, mine], dst_ref=ref.at[dst_row, :, mine], send_sem=send.at[up, rel], recv_sem=recv.at[up, rel],
-            device_id={"sp": dev, "tp": tp if rel == 0 else other}, device_id_type=MESH)
-
-    def halo_finish(ref, send, recv):
-        for up in range(2):
-            for rel in range(2):
-                dst_row, dev = (0, prv) if up == 0 else (rows + 1, nxt)
-                part = ref.at[dst_row, :, mine if rel == 0 else theirs]
-                pltpu.make_async_remote_copy(
-                    src_ref=part, dst_ref=part, send_sem=send.at[up, rel], recv_sem=recv.at[up, rel],
-                    device_id={"sp": dev, "tp": tp if rel == 0 else other}, device_id_type=MESH).wait_recv()
-
-        @pl.when(sp == 0)
-        def _():
-            ref[0] = jnp.zeros((8, 64, 128), BF16)
-
-        @pl.when(sp == row_devs - 1)
-        def _():
-            ref[rows + 1] = jnp.zeros((8, 64, 128), BF16)
-
-    def g_pair(c, sl):
-        return remote(g_all, c * 8 + 1, 8, sl, gx_send.at[c], gx_recv.at[c])
-
-    def z_pair(g, part, sl):
-        lo = lax.rem(8 * g + part * 4 + rows - 4, rows) + 1
-        return remote(z_all, lo, 4, sl, zx_send.at[g, part], zx_recv.at[g, part])
-
-    pl.semaphore_wait(barrier, len(targets))
-
-    def pack_rows(c):
-        for h in range(8):
-            for j in range(8):
-                g_all[c * 8 + h + 1, j, mine] = packed(raw_g, c * 8 + h, j)
-
-    def pack_g(c, carry):
-        load_g(c).wait()
-        pack_rows(c)
-
-        @pl.when(c == 0)
-        def _():
-            for rel in range(2):
-                halo(g_all, 1, rel, gh_send, gh_recv).start()
-
-        g_pair(c, mine).start()
-
-        @pl.when(c + ahead < n_groups)
-        def _():
-            load_g(c + ahead).start()
-
-        load_a(c + 1).start()
-        return carry
-
-    ahead = min(3, n_groups - 1)
-    lax.fori_loop(0, ahead, pack_g, 0)
-    for c in range(ahead + 1, n_groups):
-        load_a(c).start()
-    load_x.start()
-
-    def conv_tile(src, wm, b, q):
-        tile = jnp.concatenate([src[pl.ds(2 * b, 4), 2 * q + s].reshape(256, 128) for s in range(2)], axis=1)
-        d = jnp.dot(wm[...], tile, preferred_element_type=F32)
-        outs = []
-        for s in range(2):
-            part = d[:, s * 128:(s + 1) * 128]
-            outs.append(part[64:128] + pltpu.roll(part[0:64], 127, 1) + pltpu.roll(part[128:192], 1, 1))
-        return outs
-
-    def shifted(tiles):
-        left = jnp.concatenate([pltpu.roll(t, 1, 1) for t in tiles], axis=1)
-        right = jnp.concatenate([pltpu.roll(t, 127, 1) for t in tiles], axis=1)
-        return jnp.concatenate([left, jnp.concatenate(tiles, axis=1), right], axis=0)
-
-    def kgrad(tiles, gref, b):
-        rhs = jnp.concatenate([gref[pl.ds(2 * b, 4), j].reshape(256, 128) for j in range(8)], axis=1)
-        return lax.dot_general(shifted(tiles), rhs, (((1,), (1,)), ((), ())), preferred_element_type=F32)
-
-    def group_blocks(g):
-        return [lax.rem(4 * g + k + n_blocks - 2, n_blocks) for k in range(4)]
-
-    def middle(i, ahead):
-        if ahead:
-            load_g(i + ahead).wait()
-
-        @pl.when(i + 1 < n_groups)
-        def _():
-            load_a(i + 1).wait()
-            g_pair(i + 1, theirs).wait_recv()
-
-        if ahead:
-            pack_rows(i + ahead)
-        g = lax.rem(i + 1, n_groups)
-        bsum = None
-        dw = None
-        for b in group_blocks(g):
-            tiles = [jnp.concatenate([packed(raw_a, 2 * b + r, j) for r in range(2)], axis=0) for j in range(8)]
-            for q in range(4):
-                for s, o in enumerate(conv_tile(g_all, wm_two, b, q)):
-                    j = 2 * q + s
-                    m = jnp.where(tiles[j].astype(F32) > 0, o, 0.0)
-                    bsum = m if bsum is None else bsum + m
-                    z = m.astype(BF16)
-                    for r in range(2):
-                        z_all[2 * b + 1 + r, j, mine] = z[r * 32:(r + 1) * 32]
-            part = kgrad(tiles, g_all, b)
-            dw = part if dw is None else dw + part
-        bacc[...] += bsum
-        acc[...] += dw
-        if ahead:
-            g_pair(i + ahead, mine).start()
-
-            @pl.when(i + ahead == n_groups - 1)
-            def _():
-                for rel in range(2):
-                    halo(g_all, 0, rel, gh_send, gh_recv).start()
-
-        for part in range(2):
-            z_pair(g, part, mine).start()
-
     load_a(0).wait()
     g_pair(0, theirs).wait_recv()
 
@@ -237,8 +234,11 @@
 
     def reduce_begin(i):
         for t in range(3):
-            top = acc[pl.ds(t * 64, 32), :]
-            low = acc[pl.ds(t * 64 + 32, 32), :]
+            top = acc[0, pl.ds(t * 64, 32), :]
+            low = acc[0, pl.ds(t * 64 + 32, 32), :]
+            for slot in range(1, 4):
+                top = top + acc[slot, pl.ds(t * 64, 32), :]
+                low = low + acc[slot, pl.ds(t * 64 + 32, 32), :]
             e = top[:, 0:192] + low[:, 64:256]
             red[i, 0, t, coords[t], pl.ds(0, 32)] = e[:, 0:128]
             red[i, 0, t, coords[t], pl.ds(32, 16)] = jnp.concatenate([e[0:16, 128:192], e[16:32, 128:192]], axis=1)
@@ -279,28 +279,30 @@
             z_pair(g, part, theirs).wait_recv()
 
     def tail_grad(i, carry):
-        @pl.when((i > 0) & (i < n_groups - 2))
-        def _():
-            z_wait(lax.rem(i + 3, n_groups))
-
-        @pl.when(i == n_groups - 2)
+        @pl.when((i > 0) & (i < n_groups // 2 - 1))
+        def _():
+            for k in range(2):
+                z_wait(lax.rem(2 * i + 3 + k, n_groups))
+
+        @pl.when(i == n_groups // 2 - 1)
         def _():
             halo_finish(z_all, zh_send, zh_recv)
 
         dw = None
-        for b in group_blocks(lax.rem(i + 2, n_groups)):
-            tiles = [jnp.concatenate([packed(raw_x, 2 * b + r, j) for r in range(2)], axis=0) for j in range(8)]
-            part = kgrad(tiles, z_all, b)
-            dw = part if dw is None else dw + part
-        acc[...] += dw
+        for k in range(2):
+            for b in group_blocks(lax.rem(2 * i + 2 + k, n_groups)):
+                tiles = [jnp.concatenate([packed(raw_x, 2 * b + r, j) for r in range(2)], axis=0) for j in range(8)]
+                part = kgrad(tiles, z_all, b)
+                dw = part if dw is None else dw + part
+        acc[0] += dw
         return carry
 
     load_x.wait()
-    for g in range(1, min(4, n_groups)):
-        z_wait(g)
-    lax.fori_loop(0, n_groups - 2, tail_grad, 0)
+    for g in range(1, 5):
+        z_wait(g % n_groups)
+    lax.fori_loop(0, n_groups // 2 - 1, tail_grad, 0)
     reduce_step(1, 0)
-    lax.fori_loop(n_groups - 2, n_groups, tail_grad, 0)
+    lax.fori_loop(n_groups // 2 - 1, n_groups // 2, tail_grad, 0)
     reduce_begin(0)
 
     def last(c, carry):
@@ -316,16 +318,23 @@
                         dx_hbm[j + 8, 2 * b + r] = v[:, 64:120]
         return carry
 
+    def reduce_sent(i, p):
+        for t in range(3):
+            for k in range(1, side):
+                reduce_copy(i, p, t, k, coords[(p + t) % 3]).wait_send()
+
     third = max(n_groups // 3, 1)
     lax.fori_loop(0, third, last, 0)
     reduce_step(1, 1)
+    for p in range(2):
+        reduce_sent(1, p)
     reduce_step(0, 0)
     lax.fori_loop(third, min(2 * third, n_groups), last, 0)
     reduce_step(1, 2)
+    reduce_sent(1, 2)
+    reduce_sent(0, 0)
     reduce_step(0, 1)
     lax.fori_loop(min(2 * third, n_groups), n_groups, last, 0)
-    reduce_step(0, 2)
-
     for c in range(n_groups):
         g_pair(c, mine).wait_send()
         for part in range(2):
@@ -334,11 +343,9 @@
         for rel in range(2):
             halo(g_all, up, rel, gh_send, gh_recv).wait_send()
             halo(z_all, up, rel, zh_send, zh_recv).wait_send()
-    for i in range(2):
-        for p in range(3):
-            for t in range(3):
-                for k in range(1, side):
-                    reduce_copy(i, p, t, k, coords[(p + t) % 3]).wait_send()
+    reduce_sent(0, 1)
+    reduce_sent(0, 2)
+    reduce_step(0, 2)
 
 
 def write_out(*refs):
@@ -375,7 +382,7 @@
             scratch_shapes=[
                 raw, raw, raw, full, full, pltpu.VMEM((2, 3, 3, 32, 64), BF16),
                 pltpu.VMEM((192, 256), BF16), pltpu.VMEM((192, 256), BF16),
-                pltpu.VMEM((192, 256), F32), pltpu.VMEM((64, 128), F32),
+                pltpu.VMEM((4, 192, 256), F32), pltpu.VMEM((64, 128), F32),
                 pltpu.VMEM((2, 3, 3, side, 56, 128), F32),
                 dma((n_groups,)), dma((n_groups,)), dma, dma((2,)),
                 dma((n_groups,)), dma((n_groups,)), dma((2, 2)), dma((2, 2)),

time: 50.6 us -> 49.3 us (0.974); the launches traced: 49.8 us -> 49.2 us
  Pallas kernels: 49.2 us -> 48.5 us
    pallas_call x1, Pallas kernels: 46.4 us -> 45.7 us  [local_step(): pl.pallas_call(functools.partial(body, side, rows), out_shape=(pltpu.VMEM...]
where the time goes in v5:
time: 49.3 us; the launch traced here: 49.2 us
  Pallas kernels  48.5 us (98%)
  between operations  0.64 us (1%)
    pallas_call x1, Pallas kernels, local_step(): pl.pallas_call(functools.partial(body, side, rows), out_shape=(pltpu.VMEM...  45.7 us
    pallas_call x1, Pallas kernels, local_step(): pl.pallas_call(write_out, out_shape=tuple((jax.ShapeDtypeStruct(v.shape,...  2.82 us

profile of v5, /device:TPU:0, one launch (start us, length us, event | category | flops | bytes accessed | tf_op | source)
XLA Modules:
  0.0 49.2 jit_solution(2228875790645487394)
XLA Ops:
  0.6 45.7 %resblock_bwd.1 = (bf16[16,48,32,56]{3,2,1,0:T(8,128)(2,1)S(1)}, f32[3,3,32,64]{3,2,1,0:T(8,128)S(1)}, f32[3,3,32,64]{3,2,1,0:T(8,128)S(1)}, f32[1,32]{1,0:T(1,128)S(1)}) custom-call(bf16[16,48,32,56]{3,2,1,0:T(8,128)(2,1)} %bitcast.5, bf16[16,48,32,56]{3,2,1,0:T(8,128)(2,1)} %bitcast.6, bf16[16,48,32,56]{3,2,1,0:T(8,128)(2,1)} %bitcast.7, ...), custom_call_target="tpu_custom_call" | custom-call | tf_op jit(solution)/shard_map/resblock_bwd/pallas_call | solution.py:372
  46.4 2.8 %write_out.1 = (bf16[16,48,32,56]{3,2,1,0:T(8,128)(2,1)}, f32[3,3,32,64]{3,2,1,0:T(8,128)}, f32[3,3,32,64]{3,2,1,0:T(8,128)}, f32[1,32]{1,0:T(1,128)}) custom-call(bf16[16,48,32,56]{3,2,1,0:T(8,128)(2,1)S(1)} %get-tuple-element.12.refs_0_, f32[3,3,32,64]{3,2,1,0:T(8,128)S(1)} %get-tuple-element.13.refs_1_, f32[3,3,32,64]{3,2,1,0:T(8,128)S(1)} %get-tuple-element.14.refs_2_, ...), custom_call_target="tpu_custom_call" | custom-call | tf_op jit(solution)/shard_map/write_out/pallas_call | solution.py:396

commit v6 on v5

--- a/solution.py
+++ b/solution.py
@@ -49,7 +49,7 @@
     load_g(0).start()
     for w in load_w:
         w.start()
-    for c in range(1, min(3, n_groups)):
+    for c in range(1, 4):
         load_g(c).start()
     load_a(0).start()
 
@@ -121,16 +121,22 @@
 
         g_pair(c, mine).start()
 
-        @pl.when(c + ahead < n_groups)
-        def _():
-            load_g(c + ahead).start()
-
-        load_a(c + 1).start()
+        @pl.when(c == 0)
+        def _():
+            load_a(1).start()
+
+        @pl.when((c > 0) & (c < 3))
+        def _():
+            load_g(c + 3).start()
+
+        @pl.when(c >= 2)
+        def _():
+            load_a(c).start()
         return carry
 
-    ahead = min(3, n_groups - 1)
+    ahead = 4
     lax.fori_loop(0, ahead, pack_g, 0)
-    for c in range(ahead + 1, n_groups):
+    for c in range(ahead, n_groups):
         load_a(c).start()
     load_x.start()
 
@@ -155,41 +161,30 @@
     def group_blocks(g):
         return [lax.rem(4 * g + k + n_blocks - 2, n_blocks) for k in range(4)]
 
-    def middle(i, ahead):
-        if ahead:
-            load_g(i + ahead).wait()
-
-        @pl.when(i + 1 < n_groups)
-        def _():
-            load_a(i + 1).wait()
-            g_pair(i + 1, theirs).wait_recv()
-
-        if ahead:
-            pack_rows(i + ahead)
-        g = lax.rem(i + 1, n_groups)
+    def middle(groups, late):
+        for c in late:
+            load_g(c).wait()
+            pack_rows(c)
         bsum = None
-        for slot, b in enumerate(group_blocks(g)):
-            tiles = [jnp.concatenate([packed(raw_a, 2 * b + r, j) for r in range(2)], axis=0) for j in range(8)]
-            for q in range(4):
-                for s, o in enumerate(conv_tile(g_all, wm_two, b, q)):
-                    j = 2 * q + s
-                    m = jnp.where(tiles[j].astype(F32) > 0, o, 0.0)
-                    bsum = m if bsum is None else bsum + m
-                    z = m.astype(BF16)
-                    for r in range(2):
-                        z_all[2 * b + 1 + r, j, mine] = z[r * 32:(r + 1) * 32]
-            acc[slot % 4] += kgrad(tiles, g_all, b)
+        for at, g in enumerate(groups):
+            for k, b in enumerate(group_blocks(g)):
+                slot = 4 * at + k
+                tiles = [jnp.concatenate([packed(raw_a, 2 * b + r, j) for r in range(2)], axis=0) for j in range(8)]
+                for q in range(4):
+                    for s, o in enumerate(conv_tile(g_all, wm_two, b, q)):
+                        j = 2 * q + s
+                        m = jnp.where(tiles[j].astype(F32) > 0, o, 0.0)
+                        bsum = m if bsum is None else bsum + m
+                        z = m.astype(BF16)
+                        for r in range(2):
+                            z_all[2 * b + 1 + r, j, mine] = z[r * 32:(r + 1) * 32]
+                acc[slot % 4] += kgrad(tiles, g_all, b)
         bacc[...] += bsum
-        if ahead:
-            g_pair(i + ahead, mine).start()
-
-            @pl.when(i + ahead == n_groups - 1)
-            def _():
-                for rel in range(2):
-                    halo(g_all, 0, rel, gh_send, gh_recv).start()
-
-        for part in range(2):
-            z_pair(g, part, mine).start()
+        for c in late:
+            g_pair(c, mine).start()
+        for g in groups:
+            for part in range(2):
+                z_pair(g, part, mine).start()
 
     for i, wm in ((1, wm_two), (0, wm_one)):
         load_w[i].wait()
@@ -200,23 +195,23 @@
                     kh = r + 2 - rr
                     blocks.append(w_raw[i, kh, kw] if 0 <= kh < 3 else jnp.zeros((32, 64), BF16))
                 wm[pl.ds(kw * 64 + r * 32, 32), :] = jnp.concatenate(blocks, axis=1)
-    load_a(0).wait()
-    g_pair(0, theirs).wait_recv()
-
-    def middle_pack(i, carry):
-        middle(i, ahead)
+    for c in range(2):
+        load_a(c).wait()
+        g_pair(c, theirs).wait_recv()
+    middle([1], range(ahead, n_groups))
+    for rel in range(2):
+        halo(g_all, 0, rel, gh_send, gh_recv).start()
+
+    def middle_pair(i, carry):
+        for k in range(2):
+            load_a(2 * i + 2 + k).wait()
+            g_pair(2 * i + 2 + k, theirs).wait_recv()
+        middle([2 * i + 2, 2 * i + 3], ())
         return carry
 
-    def middle_plain(i, carry):
-        @pl.when(i == n_groups - 1)
-        def _():
-            halo_finish(g_all, gh_send, gh_recv)
-
-        middle(i, 0)
-        return carry
-
-    lax.fori_loop(0, n_groups - ahead, middle_pack, 0)
-    lax.fori_loop(n_groups - ahead, n_groups, middle_plain, 0)
+    lax.fori_loop(0, n_groups // 2 - 1, middle_pair, 0)
+    halo_finish(g_all, gh_send, gh_recv)
+    middle([0], ())
     for up in range(2):
         for rel in range(2):
             halo(z_all, up, rel, zh_send, zh_recv).start()
@@ -300,10 +295,9 @@
     load_x.wait()
     for g in range(1, 5):
         z_wait(g % n_groups)
-    lax.fori_loop(0, n_groups // 2 - 1, tail_grad, 0)
+    lax.fori_loop(0, n_groups // 2, tail_grad, 0)
+    reduce_begin(0)
     reduce_step(1, 0)
-    lax.fori_loop(n_groups // 2 - 1, n_groups // 2, tail_grad, 0)
-    reduce_begin(0)
 
     def last(c, carry):
         for k in range(4):
@@ -325,15 +319,15 @@
 
     third = max(n_groups // 3, 1)
     lax.fori_loop(0, third, last, 0)
+    reduce_step(0, 0)
     reduce_step(1, 1)
     for p in range(2):
         reduce_sent(1, p)
-    reduce_step(0, 0)
     lax.fori_loop(third, min(2 * third, n_groups), last, 0)
+    reduce_step(0, 1)
     reduce_step(1, 2)
     reduce_sent(1, 2)
     reduce_sent(0, 0)
-    reduce_step(0, 1)
     lax.fori_loop(min(2 * third, n_groups), n_groups, last, 0)
     for c in range(n_groups):
         g_pair(c, mine).wait_send()

time: 49.3 us -> 47.6 us (0.966)
  Pallas kernels: 48.5 us -> 46.7 us
    pallas_call x1, Pallas kernels: 45.7 us -> 43.8 us  [local_step(): pl.pallas_call(functools.partial(body, side, rows), out_shape=(pltpu.VMEM...]
where the time goes in v6:
time: 47.6 us; the launch traced here: 47.5 us
  Pallas kernels  46.7 us (98%)
  between operations  0.8 us (2%)
    pallas_call x1, Pallas kernels, local_step(): pl.pallas_call(functools.partial(body, side, rows), out_shape=(pltpu.VMEM...  43.8 us
    pallas_call x1, Pallas kernels, local_step(): pl.pallas_call(write_out, out_shape=tuple((jax.ShapeDtypeStruct(v.shape,...  2.82 us

profile of v6, /device:TPU:0, one launch (start us, length us, event | category | flops | bytes accessed | tf_op | source)
XLA Modules:
  0.0 47.5 jit_solution(7732194536536962060)
XLA Ops:
  0.6 43.8 %resblock_bwd.1 = (bf16[16,48,32,56]{3,2,1,0:T(8,128)(2,1)S(1)}, f32[3,3,32,64]{3,2,1,0:T(8,128)S(1)}, f32[3,3,32,64]{3,2,1,0:T(8,128)S(1)}, f32[1,32]{1,0:T(1,128)S(1)}) custom-call(bf16[16,48,32,56]{3,2,1,0:T(8,128)(2,1)} %bitcast.5, bf16[16,48,32,56]{3,2,1,0:T(8,128)(2,1)} %bitcast.6, bf16[16,48,32,56]{3,2,1,0:T(8,128)(2,1)} %bitcast.7, ...), custom_call_target="tpu_custom_call" | custom-call | tf_op jit(solution)/shard_map/resblock_bwd/pallas_call | solution.py:366
  44.5 2.8 %write_out.1 = (bf16[16,48,32,56]{3,2,1,0:T(8,128)(2,1)}, f32[3,3,32,64]{3,2,1,0:T(8,128)}, f32[3,3,32,64]{3,2,1,0:T(8,128)}, f32[1,32]{1,0:T(1,128)}) custom-call(bf16[16,48,32,56]{3,2,1,0:T(8,128)(2,1)S(1)} %get-tuple-element.12.refs_0_, f32[3,3,32,64]{3,2,1,0:T(8,128)S(1)} %get-tuple-element.13.refs_1_, f32[3,3,32,64]{3,2,1,0:T(8,128)S(1)} %get-tuple-element.14.refs_2_, ...), custom_call_target="tpu_custom_call" | custom-call | tf_op jit(solution)/shard_map/write_out/pallas_call | solution.py:390

commit v7 on v6

--- a/solution.py
+++ b/solution.py
@@ -228,20 +228,16 @@
                 reduce_copy(i, p, t, k, coords[(p + t) % 3]).start()
 
     def reduce_begin(i):
+        slots = 1 if i == 0 else 4
         for t in range(3):
             top = acc[0, pl.ds(t * 64, 32), :]
             low = acc[0, pl.ds(t * 64 + 32, 32), :]
-            for slot in range(1, 4):
+            for slot in range(1, slots):
                 top = top + acc[slot, pl.ds(t * 64, 32), :]
                 low = low + acc[slot, pl.ds(t * 64 + 32, 32), :]
             e = top[:, 0:192] + low[:, 64:256]
             red[i, 0, t, coords[t], pl.ds(0, 32)] = e[:, 0:128]
             red[i, 0, t, coords[t], pl.ds(32, 16)] = jnp.concatenate([e[0:16, 128:192], e[16:32, 128:192]], axis=1)
-            if i == 0 and t == 0:
-                both = bacc[0:32, :] + bacc[32:64, :]
-                col = jnp.sum(both, axis=1, keepdims=True)
-                row = jnp.broadcast_to(col, (32, 128)).T[0:8]
-                red[i, 0, t, coords[t], pl.ds(48, 8)] = jnp.concatenate([row, jnp.zeros((8, 96), F32)], axis=1)
         reduce_start(i, 0)
 
     def reduce_step(i, p):
@@ -267,7 +263,10 @@
             reduce_start(i, p + 1)
 
     reduce_begin(1)
-    acc[...] = jnp.zeros_like(acc)
+    acc[0] = jnp.zeros((192, 256), F32)
+    col = jnp.sum(bacc[0:32, :] + bacc[32:64, :], axis=1, keepdims=True)
+    row = jnp.broadcast_to(col, (32, 128)).T[0:8]
+    red[0, 0, 0, coords[0], pl.ds(48, 8)] = jnp.concatenate([row, jnp.zeros((8, 96), F32)], axis=1)
 
     def z_wait(g):
         for part in range(2):

time: 47.6 us -> 47.3 us (level)
  no operation moved by 1% of the time
where the time goes in v7:
time: 47.3 us; the launch traced here: 47.2 us
  Pallas kernels  46.4 us (98%)
  between operations  0.8 us (2%)
    pallas_call x1, Pallas kernels, local_step(): pl.pallas_call(functools.partial(body, side, rows), out_shape=(pltpu.VMEM...  43.6 us
    pallas_call x1, Pallas kernels, local_step(): pl.pallas_call(write_out, out_shape=tuple((jax.ShapeDtypeStruct(v.shape,...  2.82 us

profile of v7, /device:TPU:0, one launch (start us, length us, event | category | flops | bytes accessed | tf_op | source)
XLA Modules:
  0.0 47.2 jit_solution(288874341367267067)
XLA Ops:
  0.6 43.6 %resblock_bwd.1 = (bf16[16,48,32,56]{3,2,1,0:T(8,128)(2,1)S(1)}, f32[3,3,32,64]{3,2,1,0:T(8,128)S(1)}, f32[3,3,32,64]{3,2,1,0:T(8,128)S(1)}, f32[1,32]{1,0:T(1,128)S(1)}) custom-call(bf16[16,48,32,56]{3,2,1,0:T(8,128)(2,1)} %bitcast.5, bf16[16,48,32,56]{3,2,1,0:T(8,128)(2,1)} %bitcast.6, bf16[16,48,32,56]{3,2,1,0:T(8,128)(2,1)} %bitcast.7, ...), custom_call_target="tpu_custom_call" | custom-call | tf_op jit(solution)/shard_map/resblock_bwd/pallas_call | solution.py:365
  44.2 2.8 %write_out.1 = (bf16[16,48,32,56]{3,2,1,0:T(8,128)(2,1)}, f32[3,3,32,64]{3,2,1,0:T(8,128)}, f32[3,3,32,64]{3,2,1,0:T(8,128)}, f32[1,32]{1,0:T(1,128)}) custom-call(bf16[16,48,32,56]{3,2,1,0:T(8,128)(2,1)S(1)} %get-tuple-element.12.refs_0_, f32[3,3,32,64]{3,2,1,0:T(8,128)S(1)} %get-tuple-element.13.refs_1_, f32[3,3,32,64]{3,2,1,0:T(8,128)S(1)} %get-tuple-element.14.refs_2_, ...), custom_call_target="tpu_custom_call" | custom-call | tf_op jit(solution)/shard_map/write_out/pallas_call | solution.py:389

commit v8 on v7

--- a/solution.py
+++ b/solution.py
@@ -222,8 +222,8 @@
         return pltpu.make_async_remote_copy(src_ref=ref, dst_ref=ref, send_sem=ar_send.at[i, p, t, k - 1], recv_sem=ar_recv.at[i, p, t, k - 1],
                                             device_id={"sp": ring_peer(axis, k), "tp": tp}, device_id_type=MESH)
 
-    def reduce_start(i, p):
-        for t in range(3):
+    def reduce_start(i, p, thirds=range(3)):
+        for t in thirds:
             for k in (2, 1, 3)[:side - 1] if side > 2 else (1,):
                 reduce_copy(i, p, t, k, coords[(p + t) % 3]).start()
 
@@ -252,6 +252,8 @@
                 total = total + red[i, p, t, c, pl.ds(0, n)]
             if p < 2:
                 red[i, p + 1, t, coords[(p + 1 + t) % 3], pl.ds(0, n)] = total
+                if t:
+                    reduce_start(i, p + 1, (t - 1,))
             else:
                 out = (dw_one, dw_two)[i]
                 out[2, t] = total[0:32, 0:64]
@@ -260,7 +262,7 @@
                 if i == 0 and t == 0:
                     dbias[...] = total[48:49, 0:32]
         if p < 2:
-            reduce_start(i, p + 1)
+            reduce_start(i, p + 1, (2,))
 
     reduce_begin(1)
     acc[0] = jnp.zeros((192, 256), F32)

time: 47.3 us -> 47.3 us (level)
  no operation moved by 1% of the time
where the time goes in v8:
time: 47.3 us; the launch traced here: 47.2 us
  Pallas kernels  46.4 us (98%)
  between operations  0.8 us (2%)
    pallas_call x1, Pallas kernels, local_step(): pl.pallas_call(functools.partial(body, side, rows), out_shape=(pltpu.VMEM...  43.6 us
    pallas_call x1, Pallas kernels, local_step(): pl.pallas_call(write_out, out_shape=tuple((jax.ShapeDtypeStruct(v.shape,...  2.82 us

profile of v8, /device:TPU:0, one launch (start us, length us, event | category | flops | bytes accessed | tf_op | source)
XLA Modules:
  0.0 47.2 jit_solution(4379088133576116213)
XLA Ops:
  0.6 43.6 %resblock_bwd.1 = (bf16[16,48,32,56]{3,2,1,0:T(8,128)(2,1)S(1)}, f32[3,3,32,64]{3,2,1,0:T(8,128)S(1)}, f32[3,3,32,64]{3,2,1,0:T(8,128)S(1)}, f32[1,32]{1,0:T(1,128)S(1)}) custom-call(bf16[16,48,32,56]{3,2,1,0:T(8,128)(2,1)} %bitcast.5, bf16[16,48,32,56]{3,2,1,0:T(8,128)(2,1)} %bitcast.6, bf16[16,48,32,56]{3,2,1,0:T(8,128)(2,1)} %bitcast.7, ...), custom_call_target="tpu_custom_call" | custom-call | tf_op jit(solution)/shard_map/resblock_bwd/pallas_call | solution.py:367
  44.2 2.8 %write_out.1 = (bf16[16,48,32,56]{3,2,1,0:T(8,128)(2,1)}, f32[3,3,32,64]{3,2,1,0:T(8,128)}, f32[3,3,32,64]{3,2,1,0:T(8,128)}, f32[1,32]{1,0:T(1,128)}) custom-call(bf16[16,48,32,56]{3,2,1,0:T(8,128)(2,1)S(1)} %get-tuple-element.12.refs_0_, f32[3,3,32,64]{3,2,1,0:T(8,128)S(1)} %get-tuple-element.13.refs_1_, f32[3,3,32,64]{3,2,1,0:T(8,128)S(1)} %get-tuple-element.14.refs_2_, ...), custom_call_target="tpu_custom_call" | custom-call | tf_op jit(solution)/shard_map/write_out/pallas_call | solution.py:391
